TPU v7x, 32 devices: a whole 2x2x4 slice. The times are simulated.
32 devices in a mesh: segment: 4 (over y, x), gy: 8 (over z, core).
Axes of the slice: x: 2, y: 2, z: 4, core: 2. Of those that a mesh axis runs over, the one named last changes fastest.
Arguments:
- crops: bfloat16 [2, 32, 4, 32, 128], P(None, None, None, 'gy'), may hold values from -6 to 6
- cotangent: bfloat16 [2, 32, 4, 32, 128], P(None, None, None, 'gy'), may hold values from -0.59765625 to 0.59765625
- weights: bfloat16 [4, 2, 27, 32, 32], P('segment'), may hold values from -0.375 to 0.375
Outputs:
- features: bfloat16 [4, 2, 32, 4, 32, 128], P('segment', None, None, None, 'gy')
- weight_grads: float32 [4, 2, 27, 32, 32], P('segment')
- input_grads: float32 [4, 2, 32, 4, 32, 128], P('segment', None, None, None, 'gy')
All inputs are finite; a program needn't handle non-finite values.
Results may differ from a plain program's by a relative error of at most 0.025.
Values may be sent and summed in bfloat16 or wider, within the bound.
A program may use at most 128 MiB of HBM per device.

v0:
```python
import functools

import jax
import jax.numpy as jnp
from jax import lax
from jax.experimental import pallas as pl
from jax.experimental.pallas import tpu as pltpu
from jax.sharding import PartitionSpec as P

HALO = 2


def shifted_fields(value):
    across = value.shape[1]
    lane = lax.broadcasted_iota(jnp.int32, value.shape, 1)
    left = jnp.where(lane == 0, 0.0, pltpu.roll(value, 1, 1))
    right = jnp.where(lane == across - 1, 0.0, pltpu.roll(value, across - 1, 1))
    return [v.astype(jnp.bfloat16) for v in (left, value, right)]


def fill_columns(col, planes_of, planes):
    across = col.shape[-1] // 2
    frame = col.shape[2]
    zero = jnp.zeros((frame, across), jnp.bfloat16)
    for dx in range(3):
        col[dx, 0, :, :across] = zero
        col[dx, planes, :, across:] = zero
    for z in range(planes):
        for dx, field in enumerate(shifted_fields(planes_of(z))):
            col[dx, z + 1, :, :across] = field
            col[dx, z, :, across:] = field


def build_taps(taps, compact, out_rows):
    channels = compact.shape[1]
    frame = taps.shape[2]
    for j in range(9):
        wide = jnp.concatenate(
            [
                compact[j].astype(jnp.float32),
                jnp.zeros((channels, frame - compact.shape[2]), jnp.float32),
            ],
            1,
        )
        for y in range(out_rows):
            moved = wide if y == 0 else pltpu.roll(wide, y * channels, 1)
            taps[j, y * channels : (y + 1) * channels, :] = moved.astype(jnp.bfloat16)


def convolved(taps, col, pair, low, high):
    total = None
    for dz in range(3):
        for dx in range(3):
            part = jnp.dot(
                taps[3 * dz + dx, low:high, :],
                col[dx, 2 * pair + dz],
                preferred_element_type=jnp.float32,
            )
            total = part if total is None else total + part
    return total


def logistic_of(value):
    return 1.0 / (1.0 + jnp.exp(-value))


def row_mask(channels, rows, frame_start, inside_low, inside_high, across):
    row = lax.broadcasted_iota(jnp.int32, (rows * channels, across), 0) // channels + frame_start
    return (row >= inside_low) & (row < inside_high)


def forward_kernel(
    sizes, with_skip, low_ref, mid_ref, high_ref, first_ref, second_ref, *rest
):
    channels, planes, rows, across = sizes
    if with_skip:
        skip_ref, *rest = rest
    (features_ref, next_ref, frame_ref, hidden_ref, slope1_ref, slope2_ref, col, taps) = rest
    gy = lax.axis_index("gy")
    count = lax.axis_size("gy")
    inner = rows + 2
    inside_low = jnp.where(gy == 0, HALO, 0)
    inside_high = jnp.where(gy == count - 1, rows + HALO, rows + 2 * HALO)
    for z in range(planes):
        frame_ref[z, : HALO * channels] = low_ref[z]
        frame_ref[z, HALO * channels : (HALO + rows) * channels] = mid_ref[z]
        frame_ref[z, (HALO + rows) * channels :] = high_ref[z]
    fill_columns(col, lambda z: frame_ref[z].astype(jnp.float32), planes)
    build_taps(taps, first_ref, inner)
    mask = row_mask(channels, inner, 1, inside_low, inside_high, across)
    edge = jnp.zeros((channels, across), jnp.bfloat16)
    for pair in range(planes // 2):
        pre = convolved(taps, col, pair, 0, inner * channels)
        for half in range(2):
            z = 2 * pair + half
            part = pre[:, half * across : (half + 1) * across]
            logistic = logistic_of(part)
            slope1_ref[z] = logistic * (1.0 + part * (1.0 - logistic))
            hidden_ref[z, :channels] = edge
            hidden_ref[z, channels : (inner + 1) * channels] = jnp.where(
                mask, part * logistic, 0.0
            ).astype(jnp.bfloat16)
            hidden_ref[z, (inner + 1) * channels :] = edge
    fill_columns(col, lambda z: hidden_ref[z].astype(jnp.float32), planes)
    build_taps(taps, second_ref, inner)
    for pair in range(planes // 2):
        pre = convolved(taps, col, pair, channels, (rows + 1) * channels)
        for half in range(2):
            z = 2 * pair + half
            part = pre[:, half * across : (half + 1) * across]
            logistic = logistic_of(part)
            slope2_ref[z] = logistic * (1.0 + part * (1.0 - logistic))
            leaving = (part * logistic).astype(jnp.bfloat16)
            features_ref[z] = leaving
            if with_skip:
                leaving = (
                    leaving.astype(jnp.float32) + skip_ref[z].astype(jnp.float32)
                ).astype(jnp.bfloat16)
            next_ref[z] = leaving


def backward_kernel(
    sizes, with_extra, with_next, low_ref, mid_ref, high_ref, first_ref, second_ref, slope1_ref, *rest
):
    channels, planes, rows, across = sizes
    if with_extra:
        extra_ref, *rest = rest
    if with_next:
        slope2_ref, *rest = rest
        (grads_ref, first_delta_ref, next_ref, wide, col, taps) = rest
    else:
        (grads_ref, first_delta_ref, wide, col, taps) = rest
    gy = lax.axis_index("gy")
    count = lax.axis_size("gy")
    inner = rows + 2
    inside_low = jnp.where(gy == 0, HALO, 0)
    inside_high = jnp.where(gy == count - 1, rows + HALO, rows + 2 * HALO)
    for z in range(planes):
        wide[z, : HALO * channels] = low_ref[z]
        wide[z, HALO * channels : (HALO + rows) * channels] = mid_ref[z]
        wide[z, (HALO + rows) * channels :] = high_ref[z]
    fill_columns(col, lambda z: wide[z].astype(jnp.float32), planes)
    build_taps(taps, second_ref, inner)
    mask = row_mask(channels, inner, 1, inside_low, inside_high, across)
    edge = jnp.zeros((channels, across), jnp.bfloat16)
    for pair in range(planes // 2):
        pre = convolved(taps, col, pair, 0, inner * channels)
        for half in range(2):
            z = 2 * pair + half
            part = pre[:, half * across : (half + 1) * across]
            delta = jnp.where(mask, part * slope1_ref[z], 0.0).astype(jnp.bfloat16)
            wide[z, :channels] = edge
            wide[z, channels : (inner + 1) * channels] = delta
            wide[z, (inner + 1) * channels :] = edge
            first_delta_ref[z] = delta[channels : (rows + 1) * channels]
    fill_columns(col, lambda z: wide[z].astype(jnp.float32), planes)
    build_taps(taps, first_ref, inner)
    for pair in range(planes // 2):
        pre = convolved(taps, col, pair, channels, (rows + 1) * channels)
        for half in range(2):
            z = 2 * pair + half
            value = pre[:, half * across : (half + 1) * across].astype(jnp.bfloat16)
            if with_extra:
                value = (
                    value.astype(jnp.float32) + extra_ref[z].astype(jnp.float32)
                ).astype(jnp.bfloat16)
            grads_ref[z] = value
            if with_next:
                next_ref[z] = (value.astype(jnp.float32) * slope2_ref[z]).astype(jnp.bfloat16)


def weight_kernel(sizes, frame_ref, first_ref, hidden_ref, second_ref, out_ref, columns):
    channels, planes, rows, across = sizes
    zero = jnp.zeros((channels, rows * across), jnp.bfloat16)
    for index, (source, delta) in enumerate(((frame_ref, first_ref), (hidden_ref, second_ref))):
        for z in range(planes):
            fields = shifted_fields(source[z].astype(jnp.float32))
            for dx, field in enumerate(fields):
                for dy in range(3):
                    block = jnp.concatenate(
                        [
                            field[(y + 1 + dy) * channels : (y + 2 + dy) * channels]
                            for y in range(rows)
                        ],
                        1,
                    )
                    for dz in range(3):
                        target = z + 1 - dz
                        if 0 <= target < planes:
                            tap = (9 * dz + 3 * dy + dx) * channels
                            columns[
                                tap : tap + channels,
                                target * rows * across : (target + 1) * rows * across,
                            ] = block
        for dz, target in ((0, 0), (2, planes - 1)):
            for tap in range(9 * dz, 9 * dz + 9):
                columns[
                    tap * channels : (tap + 1) * channels,
                    target * rows * across : (target + 1) * rows * across,
                ] = zero
        right = jnp.concatenate(
            [
                delta[z, y * channels : (y + 1) * channels, :]
                for z in range(planes)
                for y in range(rows)
            ],
            1,
        )
        out_ref[index] = lax.dot_general(
            right, columns[...], (((1,), (1,)), ((), ())), preferred_element_type=jnp.float32
        )


def with_halos(block, channels):
    count = lax.axis_size("gy")
    width = HALO * channels
    forward = [(i, i + 1) for i in range(count - 1)]
    backward = [(i + 1, i) for i in range(count - 1)]
    low = lax.ppermute(block[:, -width:], "gy", forward)
    high = lax.ppermute(block[:, :width], "gy", backward)
    return low, block, high


def partner(array, axis, mask):
    return lax.ppermute(array, axis, [(i, i ^ mask) for i in range(lax.axis_size(axis))])


def local(crops, cotangent, weights):
    micro_count, channels, planes, rows, across = crops.shape
    sizes = (channels, planes, rows, across)
    segment = lax.axis_index("segment")
    sections = lax.axis_size("segment")
    micro = segment % 2
    upper = segment >= 2
    inner = rows + 2
    frame = (rows + 2 * HALO) * channels
    spec = pl.BlockSpec(memory_space=pltpu.VMEM)
    bf = lambda *shape: jax.ShapeDtypeStruct(shape, jnp.bfloat16)
    fl = lambda *shape: jax.ShapeDtypeStruct(shape, jnp.float32)
    params = pltpu.CompilerParams(vmem_limit_bytes=48 * 2**20)
    column_scratch = pltpu.VMEM((3, planes + 1, frame, 2 * across), jnp.bfloat16)
    tap_scratch = pltpu.VMEM((9, inner * channels, frame), jnp.bfloat16)

    kernels = weights[0].reshape(2, 3, 3, 3, channels, channels)
    straight = jnp.transpose(kernels, (0, 1, 3, 5, 2, 4))
    turned = jnp.transpose(jnp.flip(kernels, (1, 2, 3)), (0, 1, 3, 4, 2, 5))
    compact = jnp.stack([straight, turned], 1).reshape(2, 2, 9, channels, 3 * channels)
    compact = jnp.pad(compact, ((0, 0),) * 4 + ((0, 128 - 3 * channels),))
    gathered = [compact]
    for step in range(1, sections):
        gathered.append(
            lax.ppermute(
                compact, "segment", [(i, (i + step) % sections) for i in range(sections)]
            )
        )
    gathered = jnp.stack(gathered)
    by_section = [
        lax.dynamic_index_in_dim(gathered, (segment - s) % sections, 0, keepdims=False)
        for s in range(sections)
    ]

    def arranged(field):
        mine = lax.dynamic_index_in_dim(field, micro, 0, keepdims=False)
        return jnp.transpose(mine, (1, 2, 0, 3)).reshape(planes, rows * channels, across)

    def restored(field):
        return jnp.transpose(
            field.reshape(planes, rows, channels, across), (2, 0, 1, 3)
        )

    merged = arranged(crops)
    outgoing = arranged(cotangent)
    band = (planes, rows * channels, across)
    entering = [merged]
    features, frames, hiddens, slopes1, slopes2 = [], [], [], [], []
    for s in range(sections):
        skip = entering[2 - s] if s in (1, 2) else None
        operands = list(with_halos(merged, channels)) + [by_section[s][0, 0], by_section[s][1, 0]]
        if skip is not None:
            operands.append(skip)
        leaving, merged, wide, hidden, slope1, slope2 = pl.pallas_call(
            functools.partial(forward_kernel, sizes, skip is not None),
            out_shape=(
                bf(*band),
                bf(*band),
                bf(planes, frame, across),
                bf(planes, frame, across),
                fl(planes, inner * channels, across),
                fl(*band),
            ),
            in_specs=[spec] * len(operands),
            out_specs=(spec,) * 6,
            scratch_shapes=[column_scratch, tap_scratch],
            compiler_params=params,
        )(*operands)
        entering.append(leaving)
        features.append(leaving)
        frames.append(wide)
        hiddens.append(hidden)
        slopes1.append(slope1)
        slopes2.append(slope2)

    second = (outgoing.astype(jnp.float32) * slopes2[-1]).astype(jnp.bfloat16)
    seconds = [None] * sections
    firsts = [None] * sections
    grads = [None] * sections
    for s in reversed(range(sections)):
        seconds[s] = second
        operands = list(with_halos(second, channels)) + [
            by_section[s][0, 1],
            by_section[s][1, 1],
            slopes1[s],
        ]
        outs = [bf(*band), bf(*band)]
        if s < 2:
            operands.append(grads[3 - s])
        if s > 0:
            operands.append(slopes2[s - 1])
            outs.append(bf(*band))
        result = pl.pallas_call(
            functools.partial(backward_kernel, sizes, s < 2, s > 0),
            out_shape=tuple(outs),
            in_specs=[spec] * len(operands),
            out_specs=(spec,) * len(outs),
            scratch_shapes=[
                pltpu.VMEM((planes, frame, across), jnp.bfloat16),
                column_scratch,
                tap_scratch,
            ],
            compiler_params=params,
        )(*operands)
        grads[s], firsts[s] = result[0], result[1]
        if s > 0:
            second = result[2]

    def own(values):
        pair = [jnp.where(upper, values[k + 2], values[k]) for k in range(2)]
        keep = jnp.where(micro == 0, pair[0], pair[1])
        give = jnp.where(micro == 0, pair[1], pair[0])
        return keep, give

    def weight_terms(values):
        picked = [jnp.where(upper, values[k + 2], values[k]) for k in range(2)]
        return picked

    picked = [weight_terms(v) for v in (frames, firsts, hiddens, seconds)]
    terms = []
    for k in range(2):
        terms.append(
            pl.pallas_call(
                functools.partial(weight_kernel, sizes),
                out_shape=fl(2, channels, 27 * channels),
                in_specs=[spec] * 4,
                out_specs=spec,
                scratch_shapes=[
                    pltpu.VMEM((27 * channels, planes * rows * across), jnp.bfloat16)
                ],
                compiler_params=params,
            )(*[p[k] for p in picked])
        )
    keep = jnp.where(micro == 0, terms[0], terms[1])
    give = jnp.where(micro == 0, terms[1], terms[0])
    total = keep + partner(give.astype(jnp.bfloat16), "segment", 1).astype(jnp.float32)
    count = lax.axis_size("gy")
    mask = 1
    while mask < count:
        total = total + partner(total.astype(jnp.bfloat16), "gy", mask).astype(jnp.float32)
        mask *= 2
    weight_grads = jnp.transpose(
        total.reshape(2, channels, 27, channels), (0, 2, 3, 1)
    )

    def both(values):
        keep, give = own(values)
        come = partner(give, "segment", 1)
        first = jnp.where(micro == 0, keep, come)
        last = jnp.where(micro == 0, come, keep)
        return jnp.stack([restored(first), restored(last)])

    return (
        both(features)[None],
        weight_grads[None],
        both(grads).astype(jnp.float32)[None],
    )


def solution(mesh):
    return jax.shard_map(
        local,
        mesh=mesh,
        in_specs=(
            P(None, None, None, "gy", None),
            P(None, None, None, "gy", None),
            P("segment", None, None, None, None),
        ),
        out_specs=(
            P("segment", None, None, None, "gy", None),
            P("segment", None, None, None, None),
            P("segment", None, None, None, "gy", None),
        ),
        check_vma=False,
    )
```

profile of v0, /device:TPU:0, one launch (start us, length us, event | category | flops | bytes accessed | tf_op | source)
XLA Modules:
  0.0 113.8 jit_solution(11350797566113872845)
XLA Ops:
  4.8 3.0 %collective-permute-start.2 = (bf16[2,2,9,32,128]{4,3,2,0,1:T(8,128)(2,1)S(1)}, bf16[2,2,9,32,128]{4,3,2,0,1:T(8,128)(2,1)S(1)}, u32[]{:S(2)}, u32[]{:S(2)}) collective-permute-start(bf16[2,2,9,32,128]{4,3,2,0,1:T(8,128)(2,1)S(1)} %get-tuple-element.107), channel_id=1, source_target_pairs={{0,8},{8,16},{16,24},{24,0},{1,9},{9,17},{17,25},{25,1},{2,10},{10... | collective-permute-start | bytes 884744 | tf_op jit(solution)/shard_map/ppermute | solution.py:252
  12.2 3.0 %collective-permute-start = (bf16[4,64,128]{2,1,0:T(8,128)(2,1)S(1)}, bf16[4,64,128]{2,1,0:T(8,128)(2,1)S(1)}, u32[]{:S(2)}, u32[]{:S(2)}) collective-permute-start(bf16[4,64,128]{2,1,0:T(8,128)(2,1)S(1)} %get-tuple-element.123), channel_id=1, source_target_pairs={{0,1},{1,2},{2,3},{3,4},{4,5},{5,6},{6,7},{8,9},{9,10},{10,11},{11... | collective-permute-start | bytes 196616 | tf_op jit(solution)/shard_map/ppermute | solution.py:219
  16.7 5.4 %collective-permute-done.3 = bf16[2,2,9,32,128]{4,3,2,0,1:T(8,128)(2,1)S(1)} collective-permute-done((bf16[2,2,9,32,128]{4,3,2,0,1:T(8,128)(2,1)S(1)}, bf16[2,2,9,32,128]{4,3,2,0,1:T(8,128)(2,1)S(1)}, u32[]{:S(2)}, u32[]{:S(2)}) %collective-permute-start.3) | collective-permute-done | bytes 294944 | tf_op jit(solution)/shard_map/ppermute | solution.py:252
  22.9 1.7 %shard_map.58 = (bf16[4,128,128]{2,1,0:T(8,128)(2,1)S(1)}, bf16[4,128,128]{2,1,0:T(8,128)(2,1)S(1)}, bf16[4,256,128]{2,1,0:T(8,128)(2,1)S(1)}, bf16[4,256,128]{2...) custom-call(bf16[4,64,128]{2,1,0:T(8,128)(2,1)S(1)} %collective-permute-done.low_ref, ...), custom_call_target="tpu_custom_call" | custom-call | tf_op jit(solution)/shard_map/pallas_call | solution.py:281
  25.9 3.0 %collective-permute-start.5 = (bf16[4,64,128]{2,1,0:T(8,128)(2,1)S(1)}, bf16[4,64,128]{2,1,0:T(8,128)(2,1)S(1)}, u32[]{:S(2)}, u32[]{:S(2)}) collective-permute-start(bf16[4,64,128]{2,1,0:T(8,128)(2,1)S(1)} %get-tuple-element.121), channel_id=1, source_target_pairs={{0,1},{1,2},{2,3},{3,4},{4,5},{5,6},{6,7},{8,9},{9,10},{10,11},{11... | collective-permute-start | bytes 196616 | tf_op jit(solution)/shard_map/ppermute | solution.py:219
  29.9 1.7 %shard_map.59 = (bf16[4,128,128]{2,1,0:T(8,128)(2,1)S(1)}, bf16[4,128,128]{2,1,0:T(8,128)(2,1)S(1)}, bf16[4,256,128]{2,1,0:T(8,128)(2,1)S(1)}, bf16[4,256,128]{2...) custom-call(bf16[4,64,128]{2,1,0:T(8,128)(2,1)S(1)} %collective-permute-done.5.low_ref, ...), custom_call_target="tpu_custom_call" | custom-call | tf_op jit(solution)/shard_map/pallas_call | solution.py:281
  32.9 4.2 %collective-permute-start.7 = (bf16[4,64,128]{2,1,0:T(8,128)(2,1)S(1)}, bf16[4,64,128]{2,1,0:T(8,128)(2,1)S(1)}, u32[]{:S(2)}, u32[]{:S(2)}) collective-permute-start(bf16[4,64,128]{2,1,0:T(8,128)(2,1)S(1)} %get-tuple-element.119), channel_id=1, source_target_pairs={{0,1},{1,2},{2,3},{3,4},{4,5},{5,6},{6,7},{8,9},{9,10},{10,11},{11... | collective-permute-start | bytes 196616 | tf_op jit(solution)/shard_map/ppermute | solution.py:219
  37.9 1.7 %shard_map.60 = (bf16[4,128,128]{2,1,0:T(8,128)(2,1)S(1)}, bf16[4,128,128]{2,1,0:T(8,128)(2,1)S(1)}, bf16[4,256,128]{2,1,0:T(8,128)(2,1)S(1)}, bf16[4,256,128]{2...) custom-call(bf16[4,64,128]{2,1,0:T(8,128)(2,1)S(1)} %collective-permute-done.7.low_ref, ...), custom_call_target="tpu_custom_call" | custom-call | tf_op jit(solution)/shard_map/pallas_call | solution.py:281
  40.9 5.3 %collective-permute-start.9 = (bf16[4,64,128]{2,1,0:T(8,128)(2,1)S(1)}, bf16[4,64,128]{2,1,0:T(8,128)(2,1)S(1)}, u32[]{:S(2)}, u32[]{:S(2)}) collective-permute-start(bf16[4,64,128]{2,1,0:T(8,128)(2,1)S(1)} %get-tuple-element.117), channel_id=1, source_target_pairs={{0,1},{1,2},{2,3},{3,4},{4,5},{5,6},{6,7},{8,9},{9,10},{10,11},{11... | collective-permute-start | bytes 196616 | tf_op jit(solution)/shard_map/ppermute | solution.py:219
  47.2 2.4 %shard_map.61 = (bf16[4,128,128]{2,1,0:T(8,128)(2,1)S(1)}, bf16[4,128,128]{2,1,0:T(8,128)(2,1)}, bf16[4,256,128]{2,1,0:T(8,128)(2,1)S(1)}, bf16[4,256,128]{2,1,0...) custom-call(bf16[4,64,128]{2,1,0:T(8,128)(2,1)S(1)} %collective-permute-done.9.low_ref, ...), custom_call_target="tpu_custom_call" | custom-call | tf_op jit(solution)/shard_map/pallas_call | solution.py:281
  50.9 5.3 %collective-permute-start.12 = (bf16[4,64,128]{2,1,0:T(8,128)(2,1)S(1)}, bf16[4,64,128]{2,1,0:T(8,128)(2,1)S(1)}, u32[]{:S(2)}, u32[]{:S(2)}) collective-permute-start(bf16[4,64,128]{2,1,0:T(8,128)(2,1)S(1)} %get-tuple-element.115), channel_id=1, source_target_pairs={{0,1},{1,2},{2,3},{3,4},{4,5},{5,6},{6,7},{8,9},{9,10},{10,11},{11... | collective-permute-start | bytes 196616 | tf_op jit(solution)/shard_map/ppermute | solution.py:219
  56.2 1.8 %collective-permute-start.11 = (bf16[4,128,128]{2,1,0:T(8,128)(2,1)S(1)}, bf16[4,128,128]{2,1,0:T(8,128)(2,1)S(1)}, u32[]{:S(2)}, u32[]{:S(2)}) collective-permute-start(bf16[4,128,128]{2,1,0:T(8,128)(2,1)S(1)} %get-tuple-element.79), channel_id=1, source_target_pairs={{0,8},{8,0},{16,24},{24,16},{1,9},{9,1},{17,25},{25,17},{2,10},{10... | collective-permute-start | bytes 393224 | tf_op jit(solution)/shard_map/ppermute | solution.py:225
  60.9 4.6 %collective-permute-start.14 = (bf16[4,64,128]{2,1,0:T(8,128)(2,1)S(1)}, bf16[4,64,128]{2,1,0:T(8,128)(2,1)S(1)}, u32[]{:S(2)}, u32[]{:S(2)}) collective-permute-start(bf16[4,64,128]{2,1,0:T(8,128)(2,1)S(1)} %get-tuple-element.113), channel_id=1, source_target_pairs={{0,1},{1,2},{2,3},{3,4},{4,5},{5,6},{6,7},{8,9},{9,10},{10,11},{11... | collective-permute-start | bytes 196616 | tf_op jit(solution)/shard_map/ppermute | solution.py:219
  69.2 5.2 %collective-permute-start.16 = (bf16[4,64,128]{2,1,0:T(8,128)(2,1)S(1)}, bf16[4,64,128]{2,1,0:T(8,128)(2,1)S(1)}, u32[]{:S(2)}, u32[]{:S(2)}) collective-permute-start(bf16[4,64,128]{2,1,0:T(8,128)(2,1)S(1)} %get-tuple-element.111), channel_id=1, source_target_pairs={{0,1},{1,2},{2,3},{3,4},{4,5},{5,6},{6,7},{8,9},{9,10},{10,11},{11... | collective-permute-start | bytes 196616 | tf_op jit(solution)/shard_map/ppermute | solution.py:219
  77.9 5.3 %collective-permute-start.18 = (bf16[4,64,128]{2,1,0:T(8,128)(2,1)S(1)}, bf16[4,64,128]{2,1,0:T(8,128)(2,1)S(1)}, u32[]{:S(2)}, u32[]{:S(2)}) collective-permute-start(bf16[4,64,128]{2,1,0:T(8,128)(2,1)S(1)} %get-tuple-element.109), channel_id=1, source_target_pairs={{0,1},{1,2},{2,3},{3,4},{4,5},{5,6},{6,7},{8,9},{9,10},{10,11},{11... | collective-permute-start | bytes 196616 | tf_op jit(solution)/shard_map/ppermute | solution.py:219
  83.3 2.1 %shard_map.67 = f32[2,32,864]{2,1,0:T(8,128)S(1)} custom-call(bf16[4,256,128]{2,1,0:T(8,128)(2,1)S(1)} %broadcast_select_fusion.1.frame_ref, bf16[4,128,128]{2,1,0:T(8,128)(2,1)S(1)} %broadcast_select_fusion.7.first_ref, bf16[4,256,128]{2,1,0:T(8,128)(2,1)S(1)} %broadcast_select_fusion.hidden_ref, bf16[4,128,128]{2,1,0:T(8,128)(2,1)S(1)} %broadcast_select_fusion.6.second_ref), custom_call_target="tpu_custom_call" | custom-call | tf_op jit(solution)/shard_map/pallas_call | solution.py:350
  87.0 2.1 %shard_map.66 = f32[2,32,864]{2,1,0:T(8,128)S(1)} custom-call(bf16[4,256,128]{2,1,0:T(8,128)(2,1)S(1)} %broadcast_select_fusion.3.frame_ref, bf16[4,128,128]{2,1,0:T(8,128)(2,1)S(1)} %broadcast_select_fusion.9.first_ref, bf16[4,256,128]{2,1,0:T(8,128)(2,1)S(1)} %broadcast_select_fusion.2.hidden_ref, bf16[4,128,128]{2,1,0:T(8,128)(2,1)S(1)} %broadcast_select_fusion.8.second_ref), custom_call_target="tpu_custom_call" | custom-call | tf_op jit(solution)/shard_map/pallas_call | solution.py:350
  89.2 1.8 %collective-permute-start.20 = (bf16[2,32,864]{2,1,0:T(8,128)(2,1)S(1)}, bf16[2,32,864]{2,1,0:T(8,128)(2,1)S(1)}, u32[]{:S(2)}, u32[]{:S(2)}) collective-permute-start(bf16[2,32,864]{2,1,0:T(8,128)(2,1)S(1)} %select_convert_fusion), channel_id=1, source_target_pairs={{0,8},{8,0},{16,24},{24,16},{1,9},{9,1},{17,25},{25,17},{2,10},{10... | collective-permute-start | bytes 331784 | tf_op jit(solution)/shard_map/ppermute | solution.py:225
  91.8 2.2 %collective-permute-done.20 = bf16[2,32,864]{2,1,0:T(8,128)(2,1)S(1)} collective-permute-done((bf16[2,32,864]{2,1,0:T(8,128)(2,1)S(1)}, bf16[2,32,864]{2,1,0:T(8,128)(2,1)S(1)}, u32[]{:S(2)}, u32[]{:S(2)}) %collective-permute-start.20) | collective-permute-done | bytes 110624 | tf_op jit(solution)/shard_map/ppermute | solution.py:225
  95.4 1.8 %collective-permute-start.24 = (bf16[4,128,128]{2,1,0:T(8,128)(2,1)S(1)}, bf16[4,128,128]{2,1,0:T(8,128)(2,1)S(1)}, u32[]{:S(2)}, u32[]{:S(2)}) collective-permute-start(bf16[4,128,128]{2,1,0:T(8,128)(2,1)S(1)} %get-tuple-element.74), channel_id=1, source_target_pairs={{0,8},{8,0},{16,24},{24,16},{1,9},{9,1},{17,25},{25,17},{2,10},{10... | collective-permute-start | bytes 393224 | tf_op jit(solution)/shard_map/ppermute | solution.py:225
  97.2 3.1 %collective-permute-start.22 = (bf16[2,32,864]{2,1,0:T(8,128)(2,1)S(1)}, bf16[2,32,864]{2,1,0:T(8,128)(2,1)S(1)}, u32[]{:S(2)}, u32[]{:S(2)}) collective-permute-start(bf16[2,32,864]{2,1,0:T(8,128)(2,1)S(1)} %fusion.4), channel_id=1, source_target_pairs={{0,2},{1,3},{2,0},{3,1},{4,6},{5,7},{6,4},{7,5},{8,10},{9,11},{10,... | collective-permute-start | bytes 331784 | tf_op jit(solution)/shard_map/ppermute | solution.py:225
  101.0 2.7 %collective-permute-done.22 = bf16[2,32,864]{2,1,0:T(8,128)(2,1)S(1)} collective-permute-done((bf16[2,32,864]{2,1,0:T(8,128)(2,1)S(1)}, bf16[2,32,864]{2,1,0:T(8,128)(2,1)S(1)}, u32[]{:S(2)}, u32[]{:S(2)}) %collective-permute-start.22) | collective-permute-done | bytes 110624 | tf_op jit(solution)/shard_map/ppermute | solution.py:225
  103.8 2.8 %collective-permute-start.23 = (bf16[2,32,864]{2,1,0:T(8,128)(2,1)S(1)}, bf16[2,32,864]{2,1,0:T(8,128)(2,1)S(1)}, u32[]{:S(2)}, u32[]{:S(2)}) collective-permute-start(bf16[2,32,864]{2,1,0:T(8,128)(2,1)S(1)} %fusion.5), channel_id=1, source_target_pairs={{0,4},{1,5},{2,6},{3,7},{4,0},{5,1},{6,2},{7,3},{8,12},{9,13},{10,... | collective-permute-start | bytes 331784 | tf_op jit(solution)/shard_map/ppermute | solution.py:225
  107.6 4.3 %collective-permute-done.23 = bf16[2,32,864]{2,1,0:T(8,128)(2,1)S(1)} collective-permute-done((bf16[2,32,864]{2,1,0:T(8,128)(2,1)S(1)}, bf16[2,32,864]{2,1,0:T(8,128)(2,1)S(1)}, u32[]{:S(2)}, u32[]{:S(2)}) %collective-permute-start.23) | collective-permute-done | bytes 110624 | tf_op jit(solution)/shard_map/ppermute | solution.py:225
  (94 shorter events, 35.8 us)
Async XLA Ops:
  4.8 11.9 %collective-permute-start.2 = (bf16[2,2,9,32,128]{4,3,2,0,1:T(8,128)(2,1)S(1)}, bf16[2,2,9,32,128]{4,3,2,0,1:T(8,128)(2,1)S(1)}, u32[]{:S(2)}, u32[]{:S(2)}) collective-permute-start(bf16[2,2,9,32,128]{4,3,2,0,1:T(8,128)(2,1)S(1)} %get-tuple-element.107), channel_id=1, source_target_pairs={{0,8},{8,16},{16,24},{24,0},{1,9},{9,17},{17,25},{25,1},{2,10},{10... | collective-permute-start | bytes 884744 | tf_op jit(solution)/shard_map/ppermute | solution.py:252
  7.8 14.3 %collective-permute-start.3 = (bf16[2,2,9,32,128]{4,3,2,0,1:T(8,128)(2,1)S(1)}, bf16[2,2,9,32,128]{4,3,2,0,1:T(8,128)(2,1)S(1)}, u32[]{:S(2)}, u32[]{:S(2)}) collective-permute-start(bf16[2,2,9,32,128]{4,3,2,0,1:T(8,128)(2,1)S(1)} %get-tuple-element.107), channel_id=1, source_target_pairs={{0,16},{8,24},{16,0},{24,8},{1,17},{9,25},{17,1},{25,9},{2,18},{10... | collective-permute-start | bytes 884744 | tf_op jit(solution)/shard_map/ppermute | solution.py:252
  9.3 13.1 %collective-permute-start.4 = (bf16[2,2,9,32,128]{4,3,2,0,1:T(8,128)(2,1)S(1)}, bf16[2,2,9,32,128]{4,3,2,0,1:T(8,128)(2,1)S(1)}, u32[]{:S(2)}, u32[]{:S(2)}) collective-permute-start(bf16[2,2,9,32,128]{4,3,2,0,1:T(8,128)(2,1)S(1)} %get-tuple-element.107), channel_id=1, source_target_pairs={{0,24},{8,0},{16,8},{24,16},{1,25},{9,1},{17,9},{25,17},{2,26},{10... | collective-permute-start | bytes 884744 | tf_op jit(solution)/shard_map/ppermute | solution.py:252
  10.9 12.1 %collective-permute-start.1 = (bf16[4,64,128]{2,1,0:T(8,128)(2,1)S(1)}, bf16[4,64,128]{2,1,0:T(8,128)(2,1)S(1)}, u32[]{:S(2)}, u32[]{:S(2)}) collective-permute-start(bf16[4,64,128]{2,1,0:T(8,128)(2,1)S(1)} %get-tuple-element.122), channel_id=1, source_target_pairs={{1,0},{2,1},{3,2},{4,3},{5,4},{6,5},{7,6},{9,8},{10,9},{11,10},{12... | collective-permute-start | bytes 196616 | tf_op jit(solution)/shard_map/ppermute | solution.py:220
  12.2 10.8 %collective-permute-start = (bf16[4,64,128]{2,1,0:T(8,128)(2,1)S(1)}, bf16[4,64,128]{2,1,0:T(8,128)(2,1)S(1)}, u32[]{:S(2)}, u32[]{:S(2)}) collective-permute-start(bf16[4,64,128]{2,1,0:T(8,128)(2,1)S(1)} %get-tuple-element.123), channel_id=1, source_target_pairs={{0,1},{1,2},{2,3},{3,4},{4,5},{5,6},{6,7},{8,9},{9,10},{10,11},{11... | collective-permute-start | bytes 196616 | tf_op jit(solution)/shard_map/ppermute | solution.py:219
  24.6 4.4 %collective-permute-start.6 = (bf16[4,64,128]{2,1,0:T(8,128)(2,1)S(1)}, bf16[4,64,128]{2,1,0:T(8,128)(2,1)S(1)}, u32[]{:S(2)}, u32[]{:S(2)}) collective-permute-start(bf16[4,64,128]{2,1,0:T(8,128)(2,1)S(1)} %get-tuple-element.120), channel_id=1, source_target_pairs={{1,0},{2,1},{3,2},{4,3},{5,4},{6,5},{7,6},{9,8},{10,9},{11,10},{12... | collective-permute-start | bytes 196616 | tf_op jit(solution)/shard_map/ppermute | solution.py:220
  25.9 3.9 %collective-permute-start.5 = (bf16[4,64,128]{2,1,0:T(8,128)(2,1)S(1)}, bf16[4,64,128]{2,1,0:T(8,128)(2,1)S(1)}, u32[]{:S(2)}, u32[]{:S(2)}) collective-permute-start(bf16[4,64,128]{2,1,0:T(8,128)(2,1)S(1)} %get-tuple-element.121), channel_id=1, source_target_pairs={{0,1},{1,2},{2,3},{3,4},{4,5},{5,6},{6,7},{8,9},{9,10},{10,11},{11... | collective-permute-start | bytes 196616 | tf_op jit(solution)/shard_map/ppermute | solution.py:219
  31.6 5.5 %collective-permute-start.8 = (bf16[4,64,128]{2,1,0:T(8,128)(2,1)S(1)}, bf16[4,64,128]{2,1,0:T(8,128)(2,1)S(1)}, u32[]{:S(2)}, u32[]{:S(2)}) collective-permute-start(bf16[4,64,128]{2,1,0:T(8,128)(2,1)S(1)} %get-tuple-element.118), channel_id=1, source_target_pairs={{1,0},{2,1},{3,2},{4,3},{5,4},{6,5},{7,6},{9,8},{10,9},{11,10},{12... | collective-permute-start | bytes 196616 | tf_op jit(solution)/shard_map/ppermute | solution.py:220
  32.9 5.0 %collective-permute-start.7 = (bf16[4,64,128]{2,1,0:T(8,128)(2,1)S(1)}, bf16[4,64,128]{2,1,0:T(8,128)(2,1)S(1)}, u32[]{:S(2)}, u32[]{:S(2)}) collective-permute-start(bf16[4,64,128]{2,1,0:T(8,128)(2,1)S(1)} %get-tuple-element.119), channel_id=1, source_target_pairs={{0,1},{1,2},{2,3},{3,4},{4,5},{5,6},{6,7},{8,9},{9,10},{10,11},{11... | collective-permute-start | bytes 196616 | tf_op jit(solution)/shard_map/ppermute | solution.py:219
  39.6 6.7 %collective-permute-start.10 = (bf16[4,64,128]{2,1,0:T(8,128)(2,1)S(1)}, bf16[4,64,128]{2,1,0:T(8,128)(2,1)S(1)}, u32[]{:S(2)}, u32[]{:S(2)}) collective-permute-start(bf16[4,64,128]{2,1,0:T(8,128)(2,1)S(1)} %get-tuple-element.116), channel_id=1, source_target_pairs={{1,0},{2,1},{3,2},{4,3},{5,4},{6,5},{7,6},{9,8},{10,9},{11,10},{12... | collective-permute-start | bytes 196616 | tf_op jit(solution)/shard_map/ppermute | solution.py:220
  40.9 6.2 %collective-permute-start.9 = (bf16[4,64,128]{2,1,0:T(8,128)(2,1)S(1)}, bf16[4,64,128]{2,1,0:T(8,128)(2,1)S(1)}, u32[]{:S(2)}, u32[]{:S(2)}) collective-permute-start(bf16[4,64,128]{2,1,0:T(8,128)(2,1)S(1)} %get-tuple-element.117), channel_id=1, source_target_pairs={{0,1},{1,2},{2,3},{3,4},{4,5},{5,6},{6,7},{8,9},{9,10},{10,11},{11... | collective-permute-start | bytes 196616 | tf_op jit(solution)/shard_map/ppermute | solution.py:219
  49.6 8.5 %collective-permute-start.13 = (bf16[4,64,128]{2,1,0:T(8,128)(2,1)S(1)}, bf16[4,64,128]{2,1,0:T(8,128)(2,1)S(1)}, u32[]{:S(2)}, u32[]{:S(2)}) collective-permute-start(bf16[4,64,128]{2,1,0:T(8,128)(2,1)S(1)} %get-tuple-element.114), channel_id=1, source_target_pairs={{1,0},{2,1},{3,2},{4,3},{5,4},{6,5},{7,6},{9,8},{10,9},{11,10},{12... | collective-permute-start | bytes 196616 | tf_op jit(solution)/shard_map/ppermute | solution.py:220
  50.9 7.2 %collective-permute-start.12 = (bf16[4,64,128]{2,1,0:T(8,128)(2,1)S(1)}, bf16[4,64,128]{2,1,0:T(8,128)(2,1)S(1)}, u32[]{:S(2)}, u32[]{:S(2)}) collective-permute-start(bf16[4,64,128]{2,1,0:T(8,128)(2,1)S(1)} %get-tuple-element.115), channel_id=1, source_target_pairs={{0,1},{1,2},{2,3},{3,4},{4,5},{5,6},{6,7},{8,9},{9,10},{10,11},{11... | collective-permute-start | bytes 196616 | tf_op jit(solution)/shard_map/ppermute | solution.py:219
  56.2 18.2 %collective-permute-start.11 = (bf16[4,128,128]{2,1,0:T(8,128)(2,1)S(1)}, bf16[4,128,128]{2,1,0:T(8,128)(2,1)S(1)}, u32[]{:S(2)}, u32[]{:S(2)}) collective-permute-start(bf16[4,128,128]{2,1,0:T(8,128)(2,1)S(1)} %get-tuple-element.79), channel_id=1, source_target_pairs={{0,8},{8,0},{16,24},{24,16},{1,9},{9,1},{17,25},{25,17},{2,10},{10... | collective-permute-start | bytes 393224 | tf_op jit(solution)/shard_map/ppermute | solution.py:225
  59.6 6.0 %collective-permute-start.15 = (bf16[4,64,128]{2,1,0:T(8,128)(2,1)S(1)}, bf16[4,64,128]{2,1,0:T(8,128)(2,1)S(1)}, u32[]{:S(2)}, u32[]{:S(2)}) collective-permute-start(bf16[4,64,128]{2,1,0:T(8,128)(2,1)S(1)} %get-tuple-element.112), channel_id=1, source_target_pairs={{1,0},{2,1},{3,2},{4,3},{5,4},{6,5},{7,6},{9,8},{10,9},{11,10},{12... | collective-permute-start | bytes 196616 | tf_op jit(solution)/shard_map/ppermute | solution.py:220
  60.9 5.5 %collective-permute-start.14 = (bf16[4,64,128]{2,1,0:T(8,128)(2,1)S(1)}, bf16[4,64,128]{2,1,0:T(8,128)(2,1)S(1)}, u32[]{:S(2)}, u32[]{:S(2)}) collective-permute-start(bf16[4,64,128]{2,1,0:T(8,128)(2,1)S(1)} %get-tuple-element.113), channel_id=1, source_target_pairs={{0,1},{1,2},{2,3},{3,4},{4,5},{5,6},{6,7},{8,9},{9,10},{10,11},{11... | collective-permute-start | bytes 196616 | tf_op jit(solution)/shard_map/ppermute | solution.py:219
  67.9 6.8 %collective-permute-start.17 = (bf16[4,64,128]{2,1,0:T(8,128)(2,1)S(1)}, bf16[4,64,128]{2,1,0:T(8,128)(2,1)S(1)}, u32[]{:S(2)}, u32[]{:S(2)}) collective-permute-start(bf16[4,64,128]{2,1,0:T(8,128)(2,1)S(1)} %get-tuple-element.110), channel_id=1, source_target_pairs={{1,0},{2,1},{3,2},{4,3},{5,4},{6,5},{7,6},{9,8},{10,9},{11,10},{12... | collective-permute-start | bytes 196616 | tf_op jit(solution)/shard_map/ppermute | solution.py:220
  69.2 5.9 %collective-permute-start.16 = (bf16[4,64,128]{2,1,0:T(8,128)(2,1)S(1)}, bf16[4,64,128]{2,1,0:T(8,128)(2,1)S(1)}, u32[]{:S(2)}, u32[]{:S(2)}) collective-permute-start(bf16[4,64,128]{2,1,0:T(8,128)(2,1)S(1)} %get-tuple-element.111), channel_id=1, source_target_pairs={{0,1},{1,2},{2,3},{3,4},{4,5},{5,6},{6,7},{8,9},{9,10},{10,11},{11... | collective-permute-start | bytes 196616 | tf_op jit(solution)/shard_map/ppermute | solution.py:219
  76.6 8.8 %collective-permute-start.19 = (bf16[4,64,128]{2,1,0:T(8,128)(2,1)S(1)}, bf16[4,64,128]{2,1,0:T(8,128)(2,1)S(1)}, u32[]{:S(2)}, u32[]{:S(2)}) collective-permute-start(bf16[4,64,128]{2,1,0:T(8,128)(2,1)S(1)} %get-tuple-element.108), channel_id=1, source_target_pairs={{1,0},{2,1},{3,2},{4,3},{5,4},{6,5},{7,6},{9,8},{10,9},{11,10},{12... | collective-permute-start | bytes 196616 | tf_op jit(solution)/shard_map/ppermute | solution.py:220
  77.9 7.5 %collective-permute-start.18 = (bf16[4,64,128]{2,1,0:T(8,128)(2,1)S(1)}, bf16[4,64,128]{2,1,0:T(8,128)(2,1)S(1)}, u32[]{:S(2)}, u32[]{:S(2)}) collective-permute-start(bf16[4,64,128]{2,1,0:T(8,128)(2,1)S(1)} %get-tuple-element.109), channel_id=1, source_target_pairs={{0,1},{1,2},{2,3},{3,4},{4,5},{5,6},{6,7},{8,9},{9,10},{10,11},{11... | collective-permute-start | bytes 196616 | tf_op jit(solution)/shard_map/ppermute | solution.py:219
  89.2 4.9 %collective-permute-start.20 = (bf16[2,32,864]{2,1,0:T(8,128)(2,1)S(1)}, bf16[2,32,864]{2,1,0:T(8,128)(2,1)S(1)}, u32[]{:S(2)}, u32[]{:S(2)}) collective-permute-start(bf16[2,32,864]{2,1,0:T(8,128)(2,1)S(1)} %select_convert_fusion), channel_id=1, source_target_pairs={{0,8},{8,0},{16,24},{24,16},{1,9},{9,1},{17,25},{25,17},{2,10},{10... | collective-permute-start | bytes 331784 | tf_op jit(solution)/shard_map/ppermute | solution.py:225
  95.4 5.5 %collective-permute-start.24 = (bf16[4,128,128]{2,1,0:T(8,128)(2,1)S(1)}, bf16[4,128,128]{2,1,0:T(8,128)(2,1)S(1)}, u32[]{:S(2)}, u32[]{:S(2)}) collective-permute-start(bf16[4,128,128]{2,1,0:T(8,128)(2,1)S(1)} %get-tuple-element.74), channel_id=1, source_target_pairs={{0,8},{8,0},{16,24},{24,16},{1,9},{9,1},{17,25},{25,17},{2,10},{10... | collective-permute-start | bytes 393224 | tf_op jit(solution)/shard_map/ppermute | solution.py:225
  97.2 6.6 %collective-permute-start.22 = (bf16[2,32,864]{2,1,0:T(8,128)(2,1)S(1)}, bf16[2,32,864]{2,1,0:T(8,128)(2,1)S(1)}, u32[]{:S(2)}, u32[]{:S(2)}) collective-permute-start(bf16[2,32,864]{2,1,0:T(8,128)(2,1)S(1)} %fusion.4), channel_id=1, source_target_pairs={{0,2},{1,3},{2,0},{3,1},{4,6},{5,7},{6,4},{7,5},{8,10},{9,11},{10,... | collective-permute-start | bytes 331784 | tf_op jit(solution)/shard_map/ppermute | solution.py:225
  103.8 8.1 %collective-permute-start.23 = (bf16[2,32,864]{2,1,0:T(8,128)(2,1)S(1)}, bf16[2,32,864]{2,1,0:T(8,128)(2,1)S(1)}, u32[]{:S(2)}, u32[]{:S(2)}) collective-permute-start(bf16[2,32,864]{2,1,0:T(8,128)(2,1)S(1)} %fusion.5), channel_id=1, source_target_pairs={{0,4},{1,5},{2,6},{3,7},{4,0},{5,1},{6,2},{7,3},{8,12},{9,13},{10,... | collective-permute-start | bytes 331784 | tf_op jit(solution)/shard_map/ppermute | solution.py:225
  (4 other events, 25.5 us)
where the time goes:
time: 114 us
  starting transfers between devices  64.8 us (57%)
  waiting for transfers between devices  20.6 us (18%)
  Pallas kernels  17.6 us (15%)
  local copies, waits for them, and re-layouts  6.71 us (6%)
  other arithmetic  2.67 us (2%)
  between operations  1.38 us (1%)
    ppermute x8, starting transfers between devices, with_halos(): low = lax.ppermute(block[:, -width:], 'gy', forward)  36 us
    ppermute x6, starting transfers between devices, partner(): lax.ppermute(array, axis, [(i, i ^ mask) for i in range(lax.axis_size(axi...  12.5 us
    ppermute x8, starting transfers between devices, with_halos(): high = lax.ppermute(block[:, :width], 'gy', backward)  10.3 us
    ppermute x6, waiting for transfers between devices, partner(): lax.ppermute(array, axis, [(i, i ^ mask) for i in range(lax.axis_size(axi...  9.87 us
    pallas_call x4, Pallas kernels, local(): pl.pallas_call(functools.partial(forward_kernel, sizes, skip is not None)...  7.41 us
    ppermute x3, waiting for transfers between devices, local(): lax.ppermute(compact, 'segment', [(i, (i + step) % sections) for i in ran...  6.92 us
    ppermute x3, starting transfers between devices, local(): lax.ppermute(compact, 'segment', [(i, (i + step) % sections) for i in ran...  5.97 us
    pallas_call x4, Pallas kernels, local(): pl.pallas_call(functools.partial(backward_kernel, sizes, s < 2, s > 0), o...  5.88 us
  transfers between devices with their start and end apart: 25, of which 12 were waited for; matrix products, arithmetic and copies ran while one was open for 3% of the time, Pallas kernels for 4%

commit v1 on v0

v1 whole, which is shorter than its diff:
```python
import functools

import jax
import jax.numpy as jnp
from jax import lax
from jax.experimental import pallas as pl
from jax.experimental.pallas import tpu as pltpu
from jax.sharding import PartitionSpec as P

HALO = 2
CHUNKS = 32
MESH = pl.DeviceIdType.MESH


def logistic_of(value):
    return 0.5 + 0.5 * jnp.tanh(0.5 * value)


def shifted(value, by):
    across = value.shape[-1]
    lane = lax.broadcasted_iota(jnp.int32, value.shape, value.ndim - 1)
    if by == 1:
        return jnp.where(lane == 0, 0.0, pltpu.roll(value, 1, value.ndim - 1))
    return jnp.where(lane == across - 1, 0.0, pltpu.roll(value, across - 1, value.ndim - 1))


def network_kernel(
    sizes,
    sections,
    count,
    crop_ref,
    cot_ref,
    own_ref,
    feat_out,
    grad_out,
    wg_out,
    frame,
    hidden,
    sdelta,
    fdelta,
    slope1,
    slope2,
    feats,
    grads,
    halo,
    wbuf,
    taps,
    shifts,
    part,
    gathered,
    reduced,
    halo_send,
    halo_recv,
    w_send,
    w_recv,
    f_send,
    f_recv,
    out_send,
    out_recv,
    rs_send,
    rs_recv,
    ag_send,
    ag_recv,
):
    channels, planes, rows, across = sizes
    inner = rows + 2
    seg = lax.axis_index("segment")
    gy = lax.axis_index("gy")
    micro = seg % 2
    upper = seg // 2
    core = gy % 2
    sibling = gy + 1 - 2 * core
    partner = seg + 1 - 2 * micro
    top, bottom = HALO * channels, (HALO + rows) * channels
    has_low, has_high = gy > 0, gy < count - 1
    own_chunks = CHUNKS // count

    barrier = pltpu.get_barrier_semaphore()

    def greet(s, g):
        pl.semaphore_signal(barrier, inc=1, device_id=(s, g), device_id_type=MESH)

    for d in range(1, count):
        greet(seg, (gy + d) % count)
    for d in range(count):
        greet(partner, (gy + d) % count)
    greet((seg + 2) % sections, gy)
    greet((partner + 2) % sections, gy)

    zero_half = jnp.zeros((frame.shape[-2], across), jnp.bfloat16)
    zero_row = jnp.zeros((channels, 2 * across), jnp.bfloat16)
    for group in (frame, hidden, sdelta, fdelta):
        for s in range(group.shape[0]):
            group[s, 0, :, :across] = zero_half
            group[s, planes, :, across:] = zero_half
    for group in (hidden, fdelta):
        for s in range(group.shape[0]):
            for p in range(planes + 1):
                group[s, p, :channels] = zero_row
                group[s, p, (inner + 1) * channels :] = zero_row
    def blank(side):
        halo[:, side] = jnp.zeros(halo.shape[:1] + halo.shape[2:], jnp.bfloat16)

    pl.when(gy == 0)(lambda: blank(0))
    pl.when(gy == count - 1)(lambda: blank(1))
    part[...] = jnp.zeros(part.shape, jnp.bfloat16)
    wbuf[seg] = own_ref[...]

    def put(group, s, z, low, value):
        high = low + value.shape[0]
        group[s, z + 1, low:high, :across] = value
        group[s, z, low:high, across:] = value

    for z in range(planes):
        put(frame, 0, z, top, crop_ref[z])

    pl.semaphore_wait(barrier, 2 * count - 1 + 2)

    def halo_copy(group, s, stage, side):
        low = top if side == 1 else bottom - HALO * channels
        target = gy - 1 if side == 1 else gy + 1
        return pltpu.make_async_remote_copy(
            src_ref=group.at[s, pl.ds(1, planes), pl.ds(low, HALO * channels), pl.ds(0, across)],
            dst_ref=halo.at[stage, side],
            send_sem=halo_send.at[stage, side],
            recv_sem=halo_recv.at[stage, side],
            device_id=(seg, target),
            device_id_type=MESH,
        )

    def start_halo(group, s, stage):
        @pl.when(has_low)
        def _():
            halo_copy(group, s, stage, 1).start()

        @pl.when(has_high)
        def _():
            halo_copy(group, s, stage, 0).start()

    def finish_halo(group, s, stage):
        @pl.when(has_low)
        def _():
            halo_copy(group, s, stage, 0).wait_recv()

        @pl.when(has_high)
        def _():
            halo_copy(group, s, stage, 1).wait_recv()

        for z in range(planes):
            put(group, s, z, 0, halo[stage, 0, z])
            put(group, s, z, bottom, halo[stage, 1, z])

    def drain_halo(group, s, stage):
        @pl.when(has_low)
        def _():
            halo_copy(group, s, stage, 1).wait_send()

        @pl.when(has_high)
        def _():
            halo_copy(group, s, stage, 0).wait_send()

    def weight_copy(step, direction):
        return pltpu.make_async_remote_copy(
            src_ref=own_ref.at[direction, core],
            dst_ref=wbuf.at[seg, direction, core],
            send_sem=w_send.at[step - 1, direction],
            recv_sem=w_recv.at[step - 1, direction],
            device_id=((seg + step) % sections, gy),
            device_id_type=MESH,
        )

    def forward_copy(step, direction):
        where = wbuf.at[(seg - step + sections) % sections, direction, core]
        return pltpu.make_async_remote_copy(
            src_ref=where,
            dst_ref=where,
            send_sem=f_send.at[step - 1, direction],
            recv_sem=f_recv.at[step - 1, direction],
            device_id=(seg, sibling),
            device_id_type=MESH,
        )

    start_halo(frame, 0, 0)
    for direction in range(2):
        for step in range(1, sections):
            weight_copy(step, direction).start()

    def pass_on(s, direction):
        step = (seg - s + sections) % sections

        @pl.when(step > 0)
        def _():
            weight_copy(step, direction).wait_recv()
            forward_copy(step, direction).start()

    def arrived(s, direction):
        step = (seg - s + sections) % sections

        @pl.when(step > 0)
        def _():
            forward_copy(step, direction).wait_recv()

    def build(s, direction, conv):
        into = taps.at[s, direction, conv]
        for dz in range(3):
            for dx in range(3):
                compact = wbuf[s, direction, conv, 3 * dz + dx].astype(jnp.float32)
                wide = jnp.concatenate([compact, jnp.zeros_like(compact)], 1)
                for y in range(inner):
                    moved = wide if y == 0 else pltpu.roll(wide, y * channels, 1)
                    row = (3 * y + dx) * channels
                    into[row : row + channels, dz * 2 * across : (dz + 1) * 2 * across] = (
                        moved.astype(jnp.bfloat16)
                    )

    def convolve(s, direction, conv, group, index, pair, low, high):
        matrix = taps[s, direction, conv, 3 * low * channels : 3 * high * channels, :]
        span = group.shape[-2]
        stacked = group[index, 2 * pair : 2 * pair + 3].reshape(3 * span, 2 * across)
        full = jnp.dot(matrix, stacked, preferred_element_type=jnp.float32)
        full = full.reshape(high - low, 3, channels, 2 * across)
        halves = []
        for half in range(2):
            a, b, c = (
                full[:, dx, :, half * across : (half + 1) * across].reshape(
                    (high - low) * channels, across
                )
                for dx in range(3)
            )
            halves.append(shifted(a, 1) + b + shifted(c, -1))
        return halves

    frame_row = lax.broadcasted_iota(jnp.int32, (inner * channels, across), 0) // channels + 1
    inside_low = jnp.where(gy == 0, HALO, 0)
    inside_high = jnp.where(gy == count - 1, rows + HALO, rows + 2 * HALO)
    mask = (frame_row >= inside_low) & (frame_row < inside_high)

    def weight_terms(slot, conv, group, s, delta_group, index):
        for z in range(planes):
            delta = delta_group[index, z + 1, top:bottom, :across].astype(jnp.float32)
            for dx, field in enumerate((shifted(delta, -1), delta, shifted(delta, 1))):
                shifts[
                    z // 2,
                    dx * rows * channels : (dx + 1) * rows * channels,
                    (z % 2) * across : (z % 2 + 1) * across,
                ] = field.astype(jnp.bfloat16)
        lane = lax.broadcasted_iota(jnp.int32, (channels, across), 1) // channels
        fields = []
        for dz in range(3):
            total = None
            for pair in range(planes // 2):
                term = lax.dot_general(
                    group[s, 2 * pair + dz, channels : (inner + 1) * channels, :],
                    shifts[pair],
                    (((1,), (1,)), ((), ())),
                    preferred_element_type=jnp.float32,
                )
                total = term if total is None else total + term
            for dy in range(3):
                for dx in range(3):
                    picked = None
                    for y in range(rows):
                        block = total[
                            (y + dy) * channels : (y + dy + 1) * channels,
                            dx * rows * channels : (dx + 1) * rows * channels,
                        ]
                        picked = block if picked is None else jnp.where(lane == y, block, picked)
                    fields.append(picked)
        fields.append(jnp.zeros((channels, across), jnp.float32))
        first_half = lane < 2
        even = lane % 2 == 0
        half = across // 2
        for k in range(7):
            r = fields[4 * k : 4 * k + 4]
            pairs = [
                jnp.where(first_half, r[i], r[i + 2])
                + pltpu.roll(jnp.where(first_half, r[i + 2], r[i]), half, 1)
                for i in range(2)
            ]
            packed = jnp.where(
                even,
                pairs[0] + pltpu.roll(pairs[0], across - channels, 1),
                pairs[1] + pltpu.roll(pairs[1], channels, 1),
            ).astype(jnp.bfloat16)
            for piece in range(2):
                part[slot, 16 * conv + 2 * k + piece] = packed[16 * piece : 16 * piece + 16]

    def out_copy(source, into, kind):
        return pltpu.make_async_remote_copy(
            src_ref=source.at[partner],
            dst_ref=into.at[micro],
            send_sem=out_send.at[kind],
            recv_sem=out_recv.at[kind],
            device_id=(partner, gy),
            device_id_type=MESH,
        )

    pass_on(0, 0)
    arrived(0, 0)
    build(0, 0, 0)
    build(0, 0, 1)
    for s in range(sections):
        if s + 1 < sections:
            pass_on(s + 1, 0)
        finish_halo(frame, s, s)
        for pair in range(planes // 2):
            for half, pre in enumerate(convolve(s, 0, 0, frame, s, pair, 0, inner)):
                z = 2 * pair + half
                logistic = logistic_of(pre)
                slope1[s, z] = logistic * (1.0 + pre * (1.0 - logistic))
                put(
                    hidden, s, z, channels,
                    jnp.where(mask, pre * logistic, 0.0).astype(jnp.bfloat16),
                )
        for pair in range(planes // 2):
            for half, pre in enumerate(convolve(s, 0, 1, hidden, s, pair, 1, rows + 1)):
                z = 2 * pair + half
                logistic = logistic_of(pre)
                slope = logistic * (1.0 + pre * (1.0 - logistic))
                leaving = (pre * logistic).astype(jnp.bfloat16)
                feats[s, z] = leaving
                if s + 1 == sections:
                    second = (cot_ref[z].astype(jnp.float32) * slope).astype(jnp.bfloat16)
                    put(sdelta, s, z, top, second)
                    continue
                slope2[s, z] = slope
                if s in (1, 2):
                    skip = feats[0, z] if s == 1 else crop_ref[z]
                    leaving = (
                        leaving.astype(jnp.float32) + skip.astype(jnp.float32)
                    ).astype(jnp.bfloat16)
                put(frame, s + 1, z, top, leaving)
        if s + 1 < sections:
            start_halo(frame, s + 1, s + 1)
            arrived(s + 1, 0)
            build(s + 1, 0, 0)
            build(s + 1, 0, 1)
        else:
            start_halo(sdelta, s, sections + s)
        pass_on(sections - 1 - s, 1)

    out_copy(feats, feat_out, 0).start()
    feat_out[micro] = feats[seg]
    arrived(sections - 1, 1)
    build(sections - 1, 1, 1)
    build(sections - 1, 1, 0)
    for s in reversed(range(sections)):
        @pl.when(upper == s // 2)
        def _():
            weight_terms(s % 2, 1, hidden, s, sdelta, s)

        finish_halo(sdelta, s, sections + s)
        for pair in range(planes // 2):
            for half, pre in enumerate(convolve(s, 1, 1, sdelta, s, pair, 0, inner)):
                z = 2 * pair + half
                put(
                    fdelta, 0, z, channels,
                    jnp.where(mask, pre * slope1[s, z], 0.0).astype(jnp.bfloat16),
                )
        for pair in range(planes // 2):
            for half, pre in enumerate(convolve(s, 1, 0, fdelta, 0, pair, 1, rows + 1)):
                z = 2 * pair + half
                value = pre.astype(jnp.bfloat16)
                if s < 2:
                    value = (
                        value.astype(jnp.float32) + grads[3 - s, z].astype(jnp.float32)
                    ).astype(jnp.bfloat16)
                grads[s, z] = value
                if s > 0:
                    put(
                        sdelta, s - 1, z, top,
                        (value.astype(jnp.float32) * slope2[s - 1, z]).astype(jnp.bfloat16),
                    )
        if s > 0:
            start_halo(sdelta, s - 1, sections + s - 1)
        else:
            out_copy(grads, grad_out, 1).start()
        @pl.when(upper == s // 2)
        def _():
            weight_terms(s % 2, 0, frame, s, fdelta, 0)

        if s > 0:
            arrived(s - 1, 1)
            build(s - 1, 1, 1)
            build(s - 1, 1, 0)

    me = micro * count + gy

    def share_copy(slot, peer):
        return pltpu.make_async_remote_copy(
            src_ref=part.at[slot, pl.ds(peer * own_chunks, own_chunks)],
            dst_ref=gathered.at[me],
            send_sem=rs_send.at[slot * count + peer],
            recv_sem=rs_recv.at[me],
            device_id=(2 * upper + slot, peer),
            device_id_type=MESH,
        )

    def share_wait(sender):
        return pltpu.make_async_remote_copy(
            src_ref=part.at[0, pl.ds(0, own_chunks)],
            dst_ref=gathered.at[sender],
            send_sem=rs_send.at[0],
            recv_sem=rs_recv.at[sender],
            device_id=(partner, gy),
            device_id_type=MESH,
        )

    targets = [((micro + 1) % 2, gy)]
    for d in range(1, count):
        peer = (gy + d) % count
        targets += [(micro, peer), ((micro + 1) % 2, peer)]
    for slot, peer in targets:
        share_copy(slot, peer).start()
    grad_out[micro] = grads[seg]
    total = part[micro, pl.ds(gy * own_chunks, own_chunks)].astype(jnp.float32)
    for slot, peer in targets:
        sender = slot * count + peer
        share_wait(sender).wait_recv()
        total = total + gathered[sender].astype(jnp.float32)
    reduced[gy] = total.astype(jnp.bfloat16)

    def whole_copy(peer, owner):
        return pltpu.make_async_remote_copy(
            src_ref=reduced.at[owner],
            dst_ref=reduced.at[owner],
            send_sem=ag_send.at[peer],
            recv_sem=ag_recv.at[owner],
            device_id=(seg, peer),
            device_id_type=MESH,
        )

    peers = [(gy + d) % count for d in range(1, count)]
    for peer in peers:
        whole_copy(peer, gy).start()
    for peer in peers:
        whole_copy(peer, peer).wait_recv()
    everything = reduced[...].reshape(CHUNKS, 16, across)
    for conv in range(2):
        for t in range(27):
            k, lane_group = t // 4, t % 4
            for piece in range(2):
                block = everything[16 * conv + 2 * k + piece].astype(jnp.float32)
                if lane_group:
                    block = pltpu.roll(block, across - lane_group * channels, 1)
                wg_out[conv, t, 16 * piece : 16 * piece + 16] = block[:, :channels]

    for kind, (source, into) in enumerate(((feats, feat_out), (grads, grad_out))):
        out_copy(source, into, kind).wait()
    for s in range(sections):
        drain_halo(frame, s, s)
        drain_halo(sdelta, s, sections + s)
    for direction in range(2):
        for step in range(1, sections):
            weight_copy(step, direction).wait_send()
            forward_copy(step, direction).wait_send()
    for slot, peer in targets:
        share_copy(slot, peer).wait_send()
    for peer in peers:
        whole_copy(peer, gy).wait_send()


def local(crops, cotangent, weights):
    micro_count, channels, planes, rows, across = crops.shape
    sizes = (channels, planes, rows, across)
    segment = lax.axis_index("segment")
    sections = lax.axis_size("segment")
    count = lax.axis_size("gy")
    micro = segment % 2
    inner = rows + 2
    span = (rows + 2 * HALO) * channels
    vmem = pl.BlockSpec(memory_space=pltpu.VMEM)
    bf = lambda *shape: pltpu.VMEM(shape, jnp.bfloat16)
    fl = lambda *shape: pltpu.VMEM(shape, jnp.float32)
    dma = lambda *shape: pltpu.SemaphoreType.DMA(shape)

    kernels = weights[0].reshape(2, 3, 3, 3, channels, channels)
    straight = jnp.transpose(kernels, (0, 1, 3, 5, 2, 4))
    turned = jnp.transpose(jnp.flip(kernels, (1, 2, 3)), (0, 1, 3, 4, 2, 5))
    compact = jnp.stack([straight, turned]).reshape(2, 2, 9, channels, 3 * channels)
    compact = jnp.pad(compact, ((0, 0),) * 4 + ((0, 128 - 3 * channels),))

    def arranged(field):
        mine = lax.dynamic_index_in_dim(field, micro, 0, keepdims=False)
        return jnp.transpose(mine, (1, 2, 0, 3)).reshape(planes, rows * channels, across)

    band = (planes, rows * channels, across)
    double = (planes + 1, span, 2 * across)
    chunk = (CHUNKS // count, 16, across)
    features, grads, weight_grads = pl.pallas_call(
        functools.partial(network_kernel, sizes, sections, count),
        out_shape=(
            jax.ShapeDtypeStruct((2, *band), jnp.bfloat16),
            jax.ShapeDtypeStruct((2, *band), jnp.bfloat16),
            jax.ShapeDtypeStruct((2, 27, channels, channels), jnp.float32),
        ),
        in_specs=[vmem] * 3,
        out_specs=(vmem,) * 3,
        scratch_shapes=[
            bf(sections, *double),
            bf(sections, *double),
            bf(sections, *double),
            bf(1, *double),
            fl(sections, planes, inner * channels, across),
            fl(sections, *band),
            bf(sections, *band),
            bf(sections, *band),
            bf(2 * sections, 2, planes, HALO * channels, across),
            bf(sections, 2, 2, 9, channels, across),
            bf(sections, 2, 2, 3 * inner * channels, 3 * span),
            bf(planes // 2, 3 * rows * channels, 2 * across),
            bf(2, CHUNKS, 16, across),
            bf(2 * count, *chunk),
            bf(count, *chunk),
            dma(2 * sections, 2),
            dma(2 * sections, 2),
            dma(sections - 1, 2),
            dma(sections - 1, 2),
            dma(sections - 1, 2),
            dma(sections - 1, 2),
            dma(2),
            dma(2),
            dma(2 * count),
            dma(2 * count),
            dma(count),
            dma(count),
        ],
        compiler_params=pltpu.CompilerParams(
            vmem_limit_bytes=56 * 2**20, collective_id=0, has_side_effects=True
        ),
    )(arranged(crops), arranged(cotangent), compact)

    def restored(field):
        return jnp.transpose(
            field.reshape(2, planes, rows, channels, across), (0, 3, 1, 2, 4)
        )

    return (
        restored(features)[None],
        weight_grads[None],
        restored(grads).astype(jnp.float32)[None],
    )


def solution(mesh):
    return jax.shard_map(
        local,
        mesh=mesh,
        in_specs=(
            P(None, None, None, "gy", None),
            P(None, None, None, "gy", None),
            P("segment", None, None, None, None),
        ),
        out_specs=(
            P("segment", None, None, None, "gy", None),
            P("segment", None, None, None, None),
            P("segment", None, None, None, "gy", None),
        ),
        check_vma=False,
    )
```

time: 114 us -> 68.8 us (0.60)
  starting transfers between devices: 64.8 us -> 0 us
  Pallas kernels: 17.6 us -> 57 us
  waiting for transfers between devices: 20.6 us -> 0 us
  local copies, waits for them, and re-layouts: 6.71 us -> 10 us
  other arithmetic: 2.67 us -> 0.81 us
    ppermute x25 -> x0, starting transfers between devices: 64.8 us -> none  [the longest x8 36 us: with_halos(): low = lax.ppermute(block[:, -width:], 'gy', forward)]
    pallas_call x10 -> x1, Pallas kernels: 17.6 us -> 57 us  [local(): pl.pallas_call(functools.partial(network_kernel, sizes, sections, count),...]
    ppermute x25 -> x0, waiting for transfers between devices: 20.6 us -> none  [the longest x6 9.87 us: partner(): lax.ppermute(array, axis, [(i, i ^ mask) for i in range(lax.axis_size(axi...]
    broadcast_in_dim x0 -> x1, local copies, waits for them, and re-layouts: none -> 1.88 us  [local(): restored(grads).astype(jnp.float32)[None]]
    reshape x5 -> x1, local copies, waits for them, and re-layouts: 0.67 us -> 1.87 us  [restored(): field.reshape(2, planes, rows, channels, across)]
    convert_element_type x7 -> x0, other arithmetic: 1.17 us -> none  [the longest x1 0.96 us: local(): both(grads).astype(jnp.float32)[None]]
    unnamed x8 -> x7, local copies, waits for them, and re-layouts: 1.47 us -> 2.3 us
  transfers between devices with their start and end apart: 25 -> 0, of which waited for: 12 -> 0; matrix products, arithmetic and copies ran while one was open for 3% -> 0% of each run, Pallas kernels for 4% -> 0%
where the time goes in v1:
time: 68.8 us; the launch traced here: 68.6 us
  Pallas kernels  57 us (83%)
  local copies, waits for them, and re-layouts  10 us (15%)
  other arithmetic  0.81 us (1%)
  between operations  0.71 us (1%)
    pallas_call x1, Pallas kernels, local(): pl.pallas_call(functools.partial(network_kernel, sizes, sections, count),...  57 us
    unnamed x7, local copies, waits for them, and re-layouts  2.3 us
    broadcast_in_dim x1, local copies, waits for them, and re-layouts, local(): restored(grads).astype(jnp.float32)[None]  1.88 us
    reshape x1, local copies, waits for them, and re-layouts, restored(): field.reshape(2, planes, rows, channels, across)  1.87 us
    rev x1, local copies, waits for them, and re-layouts, local(): turned = jnp.transpose(jnp.flip(kernels, (1, 2, 3)), (0, 1, 3, 4, 2, 5))  1.57 us

profile of v1, /device:TPU:0, one launch (start us, length us, event | category | flops | bytes accessed | tf_op | source)
XLA Modules:
  0.0 68.6 jit_solution(4862229852695808883)
XLA Ops:
  0.6 0.0 copy-start
  0.7 1.1 %constant_dynamic-slice_fusion = (bf16[1,32,4,4,128]{4,3,2,1,0:T(4,128)(2,1)S(1)}, bf16[1,32,4,4,128]{4,3,2,1,0:T(4,128)(2,1)S(1)}) fusion(bf16[2,32,4,4,128]{4,3,2,1,0:T(4,128)(2,1)} %param.4, s32[]{:T(128)S(6)} %select_n.13, bf16[2,32,4,4,128]{4,3,2,1,0:T(4,128)(2,1)} %param.3), kind=kLoop, calls=%fused_computation.6 | loop fusion | bytes 524292 | tf_op jit(solution)/shard_map/jit(dynamic_index_in_dim)/dynamic_slice | solution.py:484
  1.8 0.7 %copy.17 = bf16[1,32,4,4,128]{4,1,3,2,0:T(8,128)(2,1)} copy(bf16[1,32,4,4,128]{4,3,2,1,0:T(4,128)(2,1)S(1)} %get-tuple-element.9) | data formatting | bytes 262144
  2.5 0.7 %copy.16 = bf16[1,32,4,4,128]{4,1,3,2,0:T(8,128)(2,1)} copy(bf16[1,32,4,4,128]{4,3,2,1,0:T(4,128)(2,1)S(1)} %get-tuple-element.10) | data formatting | bytes 262144
  3.2 0.0 copy-done
  3.2 0.3 copy.13
  3.5 1.6 %rev.4 = bf16[2,3,3,3,32,32]{5,2,4,3,1,0:T(4,128)(2,1)S(1)} reverse(bf16[2,3,3,3,32,32]{5,2,4,3,1,0:T(4,128)(2,1)S(1)} %copy.13), dimensions={1,2,3} | reverse | bytes 221184 | tf_op jit(solution)/shard_map/jit(_flip)/rev | solution.py:479
  5.0 0.3 stack.10
  5.3 0.5 copy.12
  5.8 0.3 stack.9
  6.1 0.8 %fusion.2.own_ref = bf16[2,2,9,32,128]{4,3,2,1,0:T(8,128)(2,1)} fusion(bf16[1,2,9,32,96]{4,3,2,1,0:T(8,128)(2,1)S(1)} %stack.10, bf16[1,2,9,32,96]{4,3,2,1,0:T(8,128)(2,1)S(1)} %stack.9), kind=kLoop, calls=%fused_computation.4 | loop fusion | flops 1032192 | bytes 516096 | tf_op jit(solution)/shard_map/stack | solution.py:480
  6.9 57.0 %shard_map.58 = (bf16[2,4,128,128]{3,2,1,0:T(8,128)(2,1)}, bf16[2,4,128,128]{3,2,1,0:T(8,128)(2,1)}, f32[2,27,32,32]{3,2,1,0:T(8,128)}) custom-call(bf16[4,128,128]{2,1,0:T(8,128)(2,1)} %bitcast.33, bf16[4,128,128]{2,1,0:T(8,128)(2,1)} %bitcast.32, bf16[2,2,9,32,128]{4,3,2,1,0:T(8,128)(2,1)} %fusion.2.own_ref), custom_call_target="tpu_custom_call" | custom-call | tf_op jit(solution)/shard_map/pallas_call | solution.py:490
  63.9 0.0 copy-start.1
  63.9 1.9 %copy.21 = bf16[2,4,4,32,128]{4,2,1,3,0:T(4,128)(2,1)} copy(bf16[2,4,4,32,128]{4,3,2,1,0:T(8,128)(2,1)} %bitcast.37) | data formatting | bytes 524288 | tf_op jit(solution)/shard_map/reshape | solution.py:535
  65.8 1.9 %copy.20 = f32[2,4,4,32,128]{4,2,1,3,0:T(4,128)} copy(bf16[2,4,4,32,128]{4,3,2,1,0:T(8,128)(2,1)} %bitcast.35) | data formatting | bytes 786432 | tf_op jit(solution)/shard_map/broadcast_in_dim | solution.py:541
  67.7 0.0 copy-done.1
  67.7 0.9 %copy.23 = f32[1,2,27,32,32]{4,3,2,1,0:T(8,128)} copy(f32[1,2,27,32,32]{4,3,2,1,0:T(8,128)S(1)} %bitcast.31) | data formatting | bytes 442368
Async XLA Ops:
  0.6 2.5 %copy-start = (bf16[1,2,27,32,32]{4,3,2,1,0:T(8,128)(2,1)S(1)}, bf16[1,2,27,32,32]{4,3,2,1,0:T(8,128)(2,1)}, u32[]{:S(2)}) copy-start(bf16[1,2,27,32,32]{4,3,2,1,0:T(8,128)(2,1)} %param.5) | copy-start | bytes 331780
  63.9 3.8 %copy-start.1 = (f32[2,27,32,32]{3,2,1,0:T(8,128)S(1)}, f32[2,27,32,32]{3,2,1,0:T(8,128)}, u32[]{:S(2)}) copy-start(f32[2,27,32,32]{3,2,1,0:T(8,128)} %get-tuple-element.7) | copy-start | bytes 663556

commit v2 on v1

v2 whole, which is shorter than its diff:
```python
import functools

import jax
import jax.numpy as jnp
from jax import lax
from jax.experimental import pallas as pl
from jax.experimental.pallas import tpu as pltpu
from jax.sharding import PartitionSpec as P

HALO = 2
PIECES = 32
PIECE_ROWS = 8
MESH = pl.DeviceIdType.MESH


def logistic_of(value):
    return 0.5 + 0.5 * jnp.tanh(0.5 * value)


def shifted(value, by):
    across = value.shape[-1]
    lane = lax.broadcasted_iota(jnp.int32, value.shape, value.ndim - 1)
    if by == 1:
        return jnp.where(lane == 0, 0.0, pltpu.roll(value, 1, value.ndim - 1))
    return jnp.where(lane == across - 1, 0.0, pltpu.roll(value, across - 1, value.ndim - 1))


def network_kernel(
    sizes,
    sections,
    count,
    crop_hbm,
    cot_hbm,
    own_hbm,
    feat_out,
    grad_out,
    reduced,
    crop_flat,
    cot_flat,
    own_ref,
    crop_ref,
    cot_ref,
    frame,
    hidden,
    sdelta,
    fdelta,
    slope1,
    slope2,
    feats,
    grads,
    halo,
    wbuf,
    taps,
    shifts,
    part,
    gathered,
    in_sem,
    halo_send,
    halo_recv,
    w_send,
    w_recv,
    f_send,
    f_recv,
    out_send,
    out_recv,
    rs_send,
    rs_recv,
    ag_send,
    ag_recv,
):
    channels, planes, rows, across = sizes
    inner = rows + 2
    seg = lax.axis_index("segment")
    gy = lax.axis_index("gy")
    micro = seg % 2
    upper = seg // 2
    core = gy % 2
    sibling = gy + 1 - 2 * core
    partner = seg + 1 - 2 * micro
    top, bottom = HALO * channels, (HALO + rows) * channels
    has_low, has_high = gy > 0, gy < count - 1
    share = PIECES // count

    loads = [
        pltpu.make_async_copy(source, into, in_sem.at[k])
        for k, (source, into) in enumerate(
            (
                (crop_hbm.at[micro], crop_flat),
                (own_hbm, own_ref),
                (cot_hbm.at[micro], cot_flat),
            )
        )
    ]
    for load in loads:
        load.start()

    def blank(side):
        halo[:, side] = jnp.zeros(halo.shape[:1] + halo.shape[2:], jnp.bfloat16)

    pl.when(gy == 0)(lambda: blank(0))
    pl.when(gy == count - 1)(lambda: blank(1))

    barrier = pltpu.get_barrier_semaphore()

    def greet(s, g):
        pl.semaphore_signal(barrier, inc=1, device_id=(s, g), device_id_type=MESH)

    for d in range(1, count):
        greet(seg, (gy + d) % count)
    for d in range(count):
        greet(partner, (gy + d) % count)
    greet((seg + 2) % sections, gy)
    greet((partner + 2) % sections, gy)

    def put(group, s, z, low, value):
        high = low + value.shape[0]
        group[s, z + 1, low:high, :across] = value
        group[s, z, low:high, across:] = value

    def by_plane(flat, z):
        size = (rows * channels, channels * planes * rows)
        place = lax.broadcasted_iota(jnp.int32, size, 0)
        source = lax.broadcasted_iota(jnp.int32, size, 1)
        wanted = (place % channels) * (planes * rows) + z * rows + place // channels
        pick = jnp.where(source == wanted, 1.0, 0.0).astype(jnp.bfloat16)
        return jnp.dot(pick, flat[...], preferred_element_type=jnp.float32).astype(jnp.bfloat16)

    loads[0].wait()
    for z in range(planes):
        plane = by_plane(crop_flat, z)
        crop_ref[z] = plane
        put(frame, 0, z, top, plane)

    pl.semaphore_wait(barrier, 2 * count - 1 + 2)

    def halo_copy(group, s, stage, side):
        low = top if side == 1 else bottom - HALO * channels
        target = gy - 1 if side == 1 else gy + 1
        return pltpu.make_async_remote_copy(
            src_ref=group.at[s, pl.ds(1, planes), pl.ds(low, HALO * channels), pl.ds(0, across)],
            dst_ref=halo.at[stage, side],
            send_sem=halo_send.at[stage, side],
            recv_sem=halo_recv.at[stage, side],
            device_id=(seg, target),
            device_id_type=MESH,
        )

    def start_halo(group, s, stage):
        @pl.when(has_low)
        def _():
            halo_copy(group, s, stage, 1).start()

        @pl.when(has_high)
        def _():
            halo_copy(group, s, stage, 0).start()

    def finish_halo(group, s, stage):
        @pl.when(has_low)
        def _():
            halo_copy(group, s, stage, 0).wait_recv()

        @pl.when(has_high)
        def _():
            halo_copy(group, s, stage, 1).wait_recv()

        for z in range(planes):
            put(group, s, z, 0, halo[stage, 0, z])
            put(group, s, z, bottom, halo[stage, 1, z])

    def drain_halo(group, s, stage):
        @pl.when(has_low)
        def _():
            halo_copy(group, s, stage, 1).wait_send()

        @pl.when(has_high)
        def _():
            halo_copy(group, s, stage, 0).wait_send()

    half_rows = channels // 2

    def weight_copy(step, direction, conv):
        return pltpu.make_async_remote_copy(
            src_ref=wbuf.at[seg, direction, conv, :, pl.ds(core * half_rows, half_rows)],
            dst_ref=wbuf.at[seg, direction, conv, :, pl.ds(core * half_rows, half_rows)],
            send_sem=w_send.at[step - 1, direction, conv],
            recv_sem=w_recv.at[step - 1, direction, conv],
            device_id=((seg + step) % sections, gy),
            device_id_type=MESH,
        )

    def weight_wait(step, direction, conv):
        where = wbuf.at[
            (seg - step + sections) % sections, direction, conv, :,
            pl.ds(core * half_rows, half_rows),
        ]
        return pltpu.make_async_remote_copy(
            src_ref=where,
            dst_ref=where,
            send_sem=w_send.at[step - 1, direction, conv],
            recv_sem=w_recv.at[step - 1, direction, conv],
            device_id=(seg, sibling),
            device_id_type=MESH,
        )

    def forward_copy(step, direction, conv, half=None):
        half = core if half is None else half
        where = wbuf.at[
            (seg - step + sections) % sections, direction, conv, :,
            pl.ds(half * half_rows, half_rows),
        ]
        return pltpu.make_async_remote_copy(
            src_ref=where,
            dst_ref=where,
            send_sem=f_send.at[step - 1, direction, conv],
            recv_sem=f_recv.at[step - 1, direction, conv],
            device_id=(seg, sibling),
            device_id_type=MESH,
        )

    def give(s, direction):
        @pl.when(seg == s)
        def _():
            for conv in (0, 1) if direction == 0 else (1, 0):
                for step in range(1, sections):
                    weight_copy(step, direction, conv).start()

    def pass_on(s, direction, conv):
        step = (seg - s + sections) % sections

        @pl.when(step > 0)
        def _():
            weight_wait(step, direction, conv).wait_recv()
            forward_copy(step, direction, conv).start()

    def arrived(s, direction, conv):
        step = (seg - s + sections) % sections

        @pl.when(step > 0)
        def _():
            forward_copy(step, direction, conv, 1 - core).wait_recv()

    start_halo(frame, 0, 0)

    loads[1].wait()
    spare = jnp.zeros((channels, across - 3 * channels), jnp.float32)
    eye = jnp.where(
        lax.broadcasted_iota(jnp.int32, (channels, channels), 0)
        == lax.broadcasted_iota(jnp.int32, (channels, channels), 1),
        1.0,
        0.0,
    ).astype(jnp.bfloat16)

    def arrange_straight(conv):
        tall = jnp.concatenate(
            [
                own_ref[conv, 9 * (j // 3) + 3 * dy + j % 3] if dy < 3
                else jnp.zeros((across - 3 * channels, channels), jnp.bfloat16)
                for j in range(9)
                for dy in range(4)
            ],
            0,
        )
        wide = lax.dot_general(
            eye, tall, (((1,), (1,)), ((), ())), preferred_element_type=jnp.float32
        ).astype(jnp.bfloat16)
        for j in range(9):
            wbuf[seg, 0, conv, j] = wide[:, j * across : (j + 1) * across]

    def arrange_turned(conv):
        for j in range(9):
            blocks = [
                own_ref[conv, 26 - (9 * (j // 3) + 3 * dy + j % 3)].astype(jnp.float32)
                for dy in range(3)
            ]
            wbuf[seg, 1, conv, j] = jnp.concatenate(blocks + [spare], 1).astype(jnp.bfloat16)

    arrange_straight(0)
    arrange_straight(1)
    give(0, 0)

    zero_half = jnp.zeros((frame.shape[-2], across), jnp.bfloat16)
    zero_row = jnp.zeros((channels, 2 * across), jnp.bfloat16)
    for group in (frame, hidden, sdelta, fdelta):
        for s in range(group.shape[0]):
            group[s, 0, :, :across] = zero_half
            group[s, planes, :, across:] = zero_half
    for group in (hidden, fdelta):
        for s in range(group.shape[0]):
            for p in range(planes + 1):
                group[s, p, :channels] = zero_row
                group[s, p, (inner + 1) * channels :] = zero_row
    for slot in range(2):
        for conv in range(2):
            for piece in range(28, PIECES):
                part[slot, conv, piece] = jnp.zeros((PIECE_ROWS, across), jnp.bfloat16)
    for conv in range(2):
        arrange_turned(conv)
    loads[2].wait()
    for z in range(planes):
        cot_ref[z] = by_plane(cot_flat, z)

    def build(s, direction, conv):
        into = taps.at[s, direction, conv]
        for dz in range(3):
            for dx in range(3):
                compact = wbuf[s, direction, conv, 3 * dz + dx].astype(jnp.float32)
                wide = jnp.concatenate([compact, jnp.zeros_like(compact)], 1)
                for y in range(inner):
                    moved = wide if y == 0 else pltpu.roll(wide, y * channels, 1)
                    row = (3 * y + dx) * channels
                    into[row : row + channels, dz * 2 * across : (dz + 1) * 2 * across] = (
                        moved.astype(jnp.bfloat16)
                    )

    def convolve(s, direction, conv, group, index, pair, low, high):
        matrix = taps[s, direction, conv, 3 * low * channels : 3 * high * channels, :]
        span = group.shape[-2]
        stacked = group[index, 2 * pair : 2 * pair + 3].reshape(3 * span, 2 * across)
        full = jnp.dot(matrix, stacked, preferred_element_type=jnp.float32)
        full = full.reshape(high - low, 3, channels, 2 * across)
        halves = []
        for half in range(2):
            a, b, c = (
                full[:, dx, :, half * across : (half + 1) * across].reshape(
                    (high - low) * channels, across
                )
                for dx in range(3)
            )
            halves.append(shifted(a, 1) + b + shifted(c, -1))
        return halves

    frame_row = lax.broadcasted_iota(jnp.int32, (inner * channels, across), 0) // channels + 1
    inside_low = jnp.where(gy == 0, HALO, 0)
    inside_high = jnp.where(gy == count - 1, rows + HALO, rows + 2 * HALO)
    mask = (frame_row >= inside_low) & (frame_row < inside_high)

    def weight_terms(slot, conv, group, s, delta_group, index):
        for z in range(planes):
            delta = delta_group[index, z + 1, top:bottom, :across].astype(jnp.float32)
            for dx, field in enumerate((shifted(delta, -1), delta, shifted(delta, 1))):
                shifts[
                    z // 2,
                    dx * rows * channels : (dx + 1) * rows * channels,
                    (z % 2) * across : (z % 2 + 1) * across,
                ] = field.astype(jnp.bfloat16)
        lane = lax.broadcasted_iota(jnp.int32, (channels, across), 1) // channels
        fields = []
        for dz in range(3):
            total = None
            for pair in range(planes // 2):
                term = lax.dot_general(
                    group[s, 2 * pair + dz, channels : (inner + 1) * channels, :],
                    shifts[pair],
                    (((1,), (1,)), ((), ())),
                    preferred_element_type=jnp.float32,
                )
                total = term if total is None else total + term
            for dy in range(3):
                for dx in range(3):
                    picked = None
                    for y in range(rows):
                        block = total[
                            (y + dy) * channels : (y + dy + 1) * channels,
                            dx * rows * channels : (dx + 1) * rows * channels,
                        ]
                        picked = block if picked is None else jnp.where(lane == y, block, picked)
                    fields.append(picked)
        fields.append(jnp.zeros((channels, across), jnp.float32))
        first_half = lane < 2
        even = lane % 2 == 0
        half = across // 2
        for k in range(7):
            r = fields[4 * k : 4 * k + 4]
            pairs = [
                jnp.where(first_half, r[i], r[i + 2])
                + pltpu.roll(jnp.where(first_half, r[i + 2], r[i]), half, 1)
                for i in range(2)
            ]
            packed = jnp.where(
                even,
                pairs[0] + pltpu.roll(pairs[0], across - channels, 1),
                pairs[1] + pltpu.roll(pairs[1], channels, 1),
            ).astype(jnp.bfloat16)
            for piece in range(4):
                part[slot, conv, 4 * k + piece] = packed[
                    piece * PIECE_ROWS : (piece + 1) * PIECE_ROWS
                ]

    def out_copy(source, into, kind):
        return pltpu.make_async_remote_copy(
            src_ref=source.at[partner],
            dst_ref=into.at[micro],
            send_sem=out_send.at[kind],
            recv_sem=out_recv.at[kind],
            device_id=(partner, gy),
            device_id_type=MESH,
        )

    me = micro * count + gy
    peers = [(gy + d) % count for d in range(1, count)]

    def share_copy(slot, conv, peer, source=None):
        source = me if source is None else source
        return pltpu.make_async_remote_copy(
            src_ref=part.at[slot, conv, pl.ds(peer * share, share)],
            dst_ref=gathered.at[conv, source],
            send_sem=rs_send.at[conv, slot * count + peer],
            recv_sem=rs_recv.at[conv, source],
            device_id=(2 * upper + slot, peer),
            device_id_type=MESH,
        )

    def send_shares(slot, conv):
        for peer in peers:
            share_copy(slot, conv, peer).start()

        @pl.when(micro != slot)
        def _():
            share_copy(slot, conv, gy).start()

    def whole_copy(conv, peer, owner):
        where = reduced.at[conv, pl.ds(owner * share, share)]
        return pltpu.make_async_remote_copy(
            src_ref=where,
            dst_ref=where,
            send_sem=ag_send.at[conv, peer],
            recv_sem=ag_recv.at[conv, owner],
            device_id=(seg, peer),
            device_id_type=MESH,
        )

    def collect(conv):
        total = part[micro, conv, pl.ds(gy * share, share)].astype(jnp.float32)
        senders = [(1 - micro) * count + gy]
        for peer in peers:
            senders += [peer, count + peer]
        for sender in senders:
            share_copy(1 - micro, conv, gy, sender).wait_recv()
            total = total + gathered[conv, sender].astype(jnp.float32)
        reduced[conv, pl.ds(gy * share, share)] = total.astype(jnp.bfloat16)
        for peer in peers:
            whole_copy(conv, peer, gy).start()

    give(1, 0)
    for conv in range(2):
        pass_on(0, 0, conv)
    for conv in range(2):
        arrived(0, 0, conv)
        build(0, 0, conv)
    for s in range(sections):
        finish_halo(frame, s, s)
        for pair in range(planes // 2):
            for half, pre in enumerate(convolve(s, 0, 0, frame, s, pair, 0, inner)):
                z = 2 * pair + half
                logistic = logistic_of(pre)
                slope1[s, z] = logistic * (1.0 + pre * (1.0 - logistic))
                put(
                    hidden, s, z, channels,
                    jnp.where(mask, pre * logistic, 0.0).astype(jnp.bfloat16),
                )
        for pair in range(planes // 2):
            for half, pre in enumerate(convolve(s, 0, 1, hidden, s, pair, 1, rows + 1)):
                z = 2 * pair + half
                logistic = logistic_of(pre)
                slope = logistic * (1.0 + pre * (1.0 - logistic))
                leaving = (pre * logistic).astype(jnp.bfloat16)
                feats[s, z] = leaving
                if s + 1 == sections:
                    second = (cot_ref[z].astype(jnp.float32) * slope).astype(jnp.bfloat16)
                    put(sdelta, s, z, top, second)
                    continue
                slope2[s, z] = slope
                if s in (1, 2):
                    skip = feats[0, z] if s == 1 else crop_ref[z]
                    leaving = (
                        leaving.astype(jnp.float32) + skip.astype(jnp.float32)
                    ).astype(jnp.bfloat16)
                put(frame, s + 1, z, top, leaving)
        if s + 1 < sections:
            start_halo(frame, s + 1, s + 1)
            if s + 2 < sections:
                give(s + 2, 0)
            give(sections - 1 - s, 1)
            for conv in range(2):
                pass_on(s + 1, 0, conv)
            for conv in range(2):
                arrived(s + 1, 0, conv)
                build(s + 1, 0, conv)
        else:
            start_halo(sdelta, s, sections + s)
            give(0, 1)
            for conv in (1, 0):
                pass_on(s, 1, conv)

    out_copy(feats, feat_out, 0).start()
    feat_out[micro] = feats[seg]
    for conv in (1, 0):
        arrived(sections - 1, 1, conv)
        build(sections - 1, 1, conv)
    for s in reversed(range(sections)):
        @pl.when(upper == s // 2)
        def _():
            weight_terms(s % 2, 1, hidden, s, sdelta, s)
            send_shares(s % 2, 1)

        if s > 0:
            for conv in (1, 0):
                pass_on(s - 1, 1, conv)

        finish_halo(sdelta, s, sections + s)
        for pair in range(planes // 2):
            for half, pre in enumerate(convolve(s, 1, 1, sdelta, s, pair, 0, inner)):
                z = 2 * pair + half
                put(
                    fdelta, 0, z, channels,
                    jnp.where(mask, pre * slope1[s, z], 0.0).astype(jnp.bfloat16),
                )
        if s == 0:
            @pl.when(upper == 0)
            def _():
                weight_terms(0, 0, frame, 0, fdelta, 0)
                send_shares(0, 0)

            collect(1)
        for pair in range(planes // 2):
            for half, pre in enumerate(convolve(s, 1, 0, fdelta, 0, pair, 1, rows + 1)):
                z = 2 * pair + half
                value = pre.astype(jnp.bfloat16)
                if s < 2:
                    value = (
                        value.astype(jnp.float32) + grads[3 - s, z].astype(jnp.float32)
                    ).astype(jnp.bfloat16)
                grads[s, z] = value
                if s > 0:
                    put(
                        sdelta, s - 1, z, top,
                        (value.astype(jnp.float32) * slope2[s - 1, z]).astype(jnp.bfloat16),
                    )
        if s > 0:
            start_halo(sdelta, s - 1, sections + s - 1)
        else:
            out_copy(grads, grad_out, 1).start()
        if s > 0:
            @pl.when(upper == s // 2)
            def _():
                weight_terms(s % 2, 0, frame, s, fdelta, 0)
                send_shares(s % 2, 0)

            for conv in (1, 0):
                arrived(s - 1, 1, conv)
                build(s - 1, 1, conv)

    grad_out[micro] = grads[seg]
    collect(0)
    for conv in (1, 0):
        for peer in peers:
            whole_copy(conv, peer, peer).wait_recv()

    for kind, (source, into) in enumerate(((feats, feat_out), (grads, grad_out))):
        out_copy(source, into, kind).wait()
    for s in range(sections):
        drain_halo(frame, s, s)
        drain_halo(sdelta, s, sections + s)
    for direction in range(2):
        for conv in range(2):
            for step in range(1, sections):
                weight_copy(step, direction, conv).wait_send()
                forward_copy(step, direction, conv).wait_send()
    for conv in range(2):
        for slot in range(2):
            for peer in peers:
                share_copy(slot, conv, peer).wait_send()
        share_copy(1 - micro, conv, gy).wait_send()
        for peer in peers:
            whole_copy(conv, peer, gy).wait_send()


def layout_kernel(
    sizes, feats, grads, reduced, feat_hbm, grad_hbm, wg_hbm, feat_flat, grad_flat, wg_wide, sems
):
    channels, planes, rows, across = sizes
    cells = channels * planes * rows
    place = lax.broadcasted_iota(jnp.int32, (cells, cells), 0)
    source = lax.broadcasted_iota(jnp.int32, (cells, cells), 1)
    wanted = (place % (planes * rows)) * channels + place // (planes * rows)
    pick = jnp.where(source == wanted, 1.0, 0.0).astype(jnp.bfloat16)
    copies = []
    everything = reduced[...].reshape(2, PIECES, PIECE_ROWS, across)
    for conv in range(2):
        for k in range(7):
            block = jnp.concatenate(
                [everything[conv, 4 * k + piece].astype(jnp.float32) for piece in range(4)], 0
            )
            for lane_group in range(4 if k < 6 else 3):
                moved = (
                    pltpu.roll(block, across - lane_group * channels, 1) if lane_group else block
                )
                wg_wide[conv, 4 * k + lane_group] = moved[:, :channels]
        copies.append(pltpu.make_async_copy(wg_wide.at[conv], wg_hbm.at[conv], sems.at[0, conv]))
        copies[-1].start()
    for k, (value, flat, hbm) in enumerate(
        ((grads, grad_flat, grad_hbm), (feats, feat_flat, feat_hbm))
    ):
        for m in range(2):
            flat[m] = jnp.dot(
                pick, value[m].reshape(cells, across), preferred_element_type=jnp.float32
            ).astype(flat.dtype)
            copies.append(pltpu.make_async_copy(flat.at[m], hbm.at[m], sems.at[k + 1, m]))
            copies[-1].start()
    for copy in copies:
        copy.wait()


def local(crops, cotangent, weights):
    micro_count, channels, planes, rows, across = crops.shape
    sizes = (channels, planes, rows, across)
    segment = lax.axis_index("segment")
    sections = lax.axis_size("segment")
    count = lax.axis_size("gy")
    micro = segment % 2
    inner = rows + 2
    span = (rows + 2 * HALO) * channels
    vmem = pl.BlockSpec(memory_space=pltpu.VMEM)
    bf = lambda *shape: pltpu.VMEM(shape, jnp.bfloat16)
    fl = lambda *shape: pltpu.VMEM(shape, jnp.float32)
    dma = lambda *shape: pltpu.SemaphoreType.DMA(shape)

    band = (planes, rows * channels, across)
    double = (planes + 1, span, 2 * across)
    cells = channels * planes * rows
    pieces = (PIECES, PIECE_ROWS, across)
    anywhere = pl.BlockSpec(memory_space=pl.ANY)
    shape = jax.ShapeDtypeStruct
    features, grads, reduced = pl.pallas_call(
        functools.partial(network_kernel, sizes, sections, count),
        out_shape=(
            shape((2, *band), jnp.bfloat16),
            shape((2, *band), jnp.bfloat16),
            shape((2, *pieces), jnp.bfloat16),
        ),
        in_specs=[anywhere] * 3,
        out_specs=(vmem,) * 3,
        scratch_shapes=[
            bf(cells, across),
            bf(cells, across),
            bf(2, 27, channels, channels),
            bf(*band),
            bf(*band),
            bf(sections, *double),
            bf(sections, *double),
            bf(sections, *double),
            bf(1, *double),
            fl(sections, planes, inner * channels, across),
            fl(sections, *band),
            bf(sections, *band),
            bf(sections, *band),
            bf(2 * sections, 2, planes, HALO * channels, across),
            bf(sections, 2, 2, 9, channels, across),
            bf(sections, 2, 2, 3 * inner * channels, 3 * span),
            bf(planes // 2, 3 * rows * channels, 2 * across),
            bf(2, 2, *pieces),
            bf(2, 2 * count, PIECES // count, PIECE_ROWS, across),
            dma(3),
            dma(2 * sections, 2),
            dma(2 * sections, 2),
            dma(sections - 1, 2, 2),
            dma(sections - 1, 2, 2),
            dma(sections - 1, 2, 2),
            dma(sections - 1, 2, 2),
            dma(2),
            dma(2),
            dma(2, 2 * count),
            dma(2, 2 * count),
            dma(2, count),
            dma(2, count),
        ],
        compiler_params=pltpu.CompilerParams(
            vmem_limit_bytes=48 * 2**20, collective_id=0, has_side_effects=True
        ),
    )(
        crops.reshape(micro_count, cells, across),
        cotangent.reshape(micro_count, cells, across),
        weights[0],
    )
    features, grads, weight_grads = pl.pallas_call(
        functools.partial(layout_kernel, sizes),
        out_shape=(
            shape((2, cells, across), jnp.bfloat16),
            shape((2, cells, across), jnp.float32),
            shape((2, 27, channels, channels), jnp.float32),
        ),
        in_specs=[vmem] * 3,
        out_specs=(anywhere,) * 3,
        scratch_shapes=[
            bf(2, cells, across),
            fl(2, cells, across),
            fl(2, 27, channels, channels),
            dma(3, 2),
        ],
        compiler_params=pltpu.CompilerParams(vmem_limit_bytes=8 * 2**20),
    )(features, grads, reduced)
    volume = (1, 2, channels, planes, rows, across)
    return features.reshape(volume), weight_grads[None], grads.reshape(volume)


def solution(mesh):
    return jax.shard_map(
        local,
        mesh=mesh,
        in_specs=(
            P(None, None, None, "gy", None),
            P(None, None, None, "gy", None),
            P("segment", None, None, None, None),
        ),
        out_specs=(
            P("segment", None, None, None, "gy", None),
            P("segment", None, None, None, None),
            P("segment", None, None, None, "gy", None),
        ),
        check_vma=False,
    )
```

time: 68.8 us -> 60.6 us (0.88)
  local copies, waits for them, and re-layouts: 10 us -> 2.91 us
  other arithmetic: 0.81 us -> 0 us
    pallas_call x1, Pallas kernels: 57 us -> 55.1 us  [local(): pl.pallas_call(functools.partial(network_kernel, sizes, sections, count),...]
    broadcast_in_dim x1 -> x0, local copies, waits for them, and re-layouts: 1.88 us -> none  [local(): restored(grads).astype(jnp.float32)[None]]
    reshape x1 -> x0, local copies, waits for them, and re-layouts: 1.87 us -> none  [restored(): field.reshape(2, planes, rows, channels, across)]
    rev x1 -> x0, local copies, waits for them, and re-layouts: 1.57 us -> none  [local(): turned = jnp.transpose(jnp.flip(kernels, (1, 2, 3)), (0, 1, 3, 4, 2, 5))]
    pallas_call x0 -> x1, Pallas kernels: none -> 1.55 us  [local(): pl.pallas_call(functools.partial(layout_kernel, sizes), out_shape=(shape(...]
    another operation x4 -> x0, local copies, waits for them, and re-layouts: 1.3 us -> none  [the longest x2 0.79 us: local(): kernels = weights[0].reshape(2, 3, 3, 3, channels, channels)]
    dynamic_slice x1 -> x0, local copies, waits for them, and re-layouts: 1.12 us -> none  [arranged(): mine = lax.dynamic_index_in_dim(field, micro, 0, keepdims=False)]
    another operation x1 -> x0, other arithmetic: 0.81 us -> none  [local(): jnp.stack([straight, turned]).reshape(2, 2, 9, channels, 3 * channels)]
where the time goes in v2:
time: 60.6 us; the launch traced here: 60.4 us
  Pallas kernels  56.7 us (94%)
  local copies, waits for them, and re-layouts  2.91 us (5%)
  between operations  0.81 us (1%)
    pallas_call x1, Pallas kernels, local(): pl.pallas_call(functools.partial(network_kernel, sizes, sections, count),...  55.1 us
    unnamed x6, local copies, waits for them, and re-layouts  2.91 us
    pallas_call x1, Pallas kernels, local(): pl.pallas_call(functools.partial(layout_kernel, sizes), out_shape=(shape(...  1.55 us

profile of v2, /device:TPU:0, one launch (start us, length us, event | category | flops | bytes accessed | tf_op | source)
XLA Modules:
  0.0 60.4 jit_solution(1978257567375879643)
XLA Ops:
  0.6 0.0 copy-start
  0.6 1.0 %copy-done = bf16[1,2,27,32,32]{4,3,2,1,0:T(8,128)(2,1)S(1)} copy-done((bf16[1,2,27,32,32]{4,3,2,1,0:T(8,128)(2,1)S(1)}, bf16[1,2,27,32,32]{4,3,2,1,0:T(8,128)(2,1)}, u32[]{:S(2)}) %copy-start) | copy-done | bytes 110616
  1.6 0.0 copy-start.1
  1.6 0.9 %copy-done.1 = bf16[2,32,4,4,128]{4,3,2,1,0:T(4,128)(2,1)S(1)} copy-done((bf16[2,32,4,4,128]{4,3,2,1,0:T(4,128)(2,1)S(1)}, bf16[2,32,4,4,128]{4,3,2,1,0:T(4,128)(2,1)}, u32[]{:S(2)}) %copy-start.1) | copy-done | bytes 262168
  2.6 0.0 copy-start.2
  2.6 0.9 %copy-done.2 = bf16[2,32,4,4,128]{4,3,2,1,0:T(4,128)(2,1)S(1)} copy-done((bf16[2,32,4,4,128]{4,3,2,1,0:T(4,128)(2,1)S(1)}, bf16[2,32,4,4,128]{4,3,2,1,0:T(4,128)(2,1)}, u32[]{:S(2)}) %copy-start.2) | copy-done | bytes 262168
  3.5 55.1 %shard_map.58 = (bf16[2,4,128,128]{3,2,1,0:T(8,128)(2,1)S(1)}, bf16[2,4,128,128]{3,2,1,0:T(8,128)(2,1)S(1)}, bf16[2,32,8,128]{3,2,1,0:T(8,128)(2,1)S(1)}) custom-call(bf16[2,512,128]{2,1,0:T(8,128)(2,1)S(1)} %bitcast.7, bf16[2,512,128]{2,1,0:T(8,128)(2,1)S(1)} %bitcast.8, bf16[2,27,32,32]{3,2,1,0:T(8,128)(2,1)S(1)} %bitcast.6), custom_call_target="tpu_custom_call" | custom-call | tf_op jit(solution)/shard_map/pallas_call | solution.py:634
  58.7 1.6 %shard_map.59 = (bf16[2,512,128]{2,1,0:T(8,128)(2,1)}, f32[2,512,128]{2,1,0:T(8,128)}, f32[2,27,32,32]{3,2,1,0:T(8,128)}) custom-call(bf16[2,4,128,128]{3,2,1,0:T(8,128)(2,1)S(1)} %get-tuple-element.9.feats, bf16[2,4,128,128]{3,2,1,0:T(8,128)(2,1)S(1)} %get-tuple-element.10.grads, bf16[2,32,8,128]{3,2,1,0:T(8,128)(2,1)S(1)} %get-tuple-element.11.reduced), custom_call_target="tpu_custom_call" | custom-call | tf_op jit(solution)/shard_map/pallas_call | solution.py:685
Async XLA Ops:
  0.6 1.0 %copy-start = (bf16[1,2,27,32,32]{4,3,2,1,0:T(8,128)(2,1)S(1)}, bf16[1,2,27,32,32]{4,3,2,1,0:T(8,128)(2,1)}, u32[]{:S(2)}) copy-start(bf16[1,2,27,32,32]{4,3,2,1,0:T(8,128)(2,1)} %param.5) | copy-start | bytes 331780
  1.6 0.9 %copy-start.1 = (bf16[2,32,4,4,128]{4,3,2,1,0:T(4,128)(2,1)S(1)}, bf16[2,32,4,4,128]{4,3,2,1,0:T(4,128)(2,1)}, u32[]{:S(2)}) copy-start(bf16[2,32,4,4,128]{4,3,2,1,0:T(4,128)(2,1)} %param.3) | copy-start | bytes 786436
  2.6 0.9 %copy-start.2 = (bf16[2,32,4,4,128]{4,3,2,1,0:T(4,128)(2,1)S(1)}, bf16[2,32,4,4,128]{4,3,2,1,0:T(4,128)(2,1)}, u32[]{:S(2)}) copy-start(bf16[2,32,4,4,128]{4,3,2,1,0:T(4,128)(2,1)} %param.4) | copy-start | bytes 786436

commit v3 on v2

v3 whole, which is shorter than its diff:
```python
import functools

import jax
import jax.numpy as jnp
from jax import lax
from jax.experimental import pallas as pl
from jax.experimental.pallas import tpu as pltpu
from jax.sharding import PartitionSpec as P

HALO = 2
PIECES = 32
PIECE_ROWS = 8
MESH = pl.DeviceIdType.MESH


def logistic_of(value):
    return 0.5 + 0.5 * jnp.tanh(0.5 * value)


def shifted(value, by):
    across = value.shape[-1]
    lane = lax.broadcasted_iota(jnp.int32, value.shape, value.ndim - 1)
    if by == 1:
        return jnp.where(lane == 0, 0.0, pltpu.roll(value, 1, value.ndim - 1))
    return jnp.where(lane == across - 1, 0.0, pltpu.roll(value, across - 1, value.ndim - 1))


def network_kernel(
    sizes,
    sections,
    count,
    crop_hbm,
    cot_hbm,
    own_hbm,
    feat_out,
    grad_out,
    reduced,
    flat,
    own_ref,
    crop_ref,
    cot_ref,
    frame,
    hidden,
    sdelta,
    fdelta,
    slope1,
    slope2,
    feats,
    grads,
    halo,
    wpack,
    taps,
    shifts,
    part,
    gathered,
    in_sem,
    know,
    halo_send,
    halo_recv,
    w_send,
    w_recv,
    f_send,
    f_recv,
    out_send,
    out_recv,
    rs_send,
    rs_recv,
    ag_send,
    ag_recv,
):
    channels, planes, rows, across = sizes
    inner = rows + 2
    seg = lax.axis_index("segment")
    gy = lax.axis_index("gy")
    micro = seg % 2
    upper = seg // 2
    core = gy % 2
    sibling = gy + 1 - 2 * core
    partner = seg + 1 - 2 * micro
    top, bottom = HALO * channels, (HALO + rows) * channels
    share = PIECES // count

    loads = [
        pltpu.make_async_copy(source, into, in_sem.at[k])
        for k, (source, into) in enumerate(
            (
                (own_hbm, own_ref),
                (crop_hbm.at[micro], flat.at[:, pl.ds(0, across)]),
                (cot_hbm.at[micro], flat.at[:, pl.ds(across, across)]),
            )
        )
    ]
    for load in loads:
        load.start()

    def blank(side):
        halo[:, side] = jnp.zeros(halo.shape[:1] + halo.shape[2:], jnp.bfloat16)

    pl.when(gy == 0)(lambda: blank(0))
    pl.when(gy == count - 1)(lambda: blank(1))

    barrier = pltpu.get_barrier_semaphore()

    def greet(s, g):
        pl.semaphore_signal(barrier, inc=1, device_id=(s, g), device_id_type=MESH)

    beside = count <= 2 * sections
    if beside:
        for by in (-1, 1):
            @pl.when((gy + by >= 0) & (gy + by < count))
            def _(by=by):
                greet(seg, gy + by)
                greet(partner, gy + by)

        greet(partner, gy)
        arrivals = 2 * (jnp.where(gy > 0, 1, 0) + jnp.where(gy < count - 1, 1, 0)) + 3
    else:
        for d in range(1, count):
            greet(seg, (gy + d) % count)
        for d in range(count):
            greet(partner, (gy + d) % count)
        arrivals = 2 * count - 1 + 2
    greet((seg + 2) % sections, gy)
    greet((partner + 2) % sections, gy)

    def neighbours():
        return jnp.where(gy > 0, 1, 0) + jnp.where(gy < count - 1, 1, 0)

    rounds = list(range(count - 2)) if beside else []

    def tell():
        if len(told) > len(heard):
            heard.append(told[-1])
            pl.semaphore_wait(know.at[heard[-1]], neighbours())
        if len(told) < len(rounds):
            told.append(len(told))
            for by in (-1, 1):
                @pl.when((gy + by >= 0) & (gy + by < count))
                def _(by=by):
                    pl.semaphore_signal(
                        know.at[told[-1]], inc=1, device_id=(seg, gy + by), device_id_type=MESH
                    )

    told, heard = [], []

    def put(group, s, z, low, value):
        at = pl.ds(low, value.shape[0])
        group[s, z + 1, at, :across] = value
        group[s, z, at, across:] = value

    zero_half = jnp.zeros((frame.shape[-2], across), jnp.bfloat16)
    zero_rows = jnp.zeros((HALO * channels, 2 * across), jnp.bfloat16)
    for group in (frame, hidden, sdelta, fdelta):
        for s in range(group.shape[0]):
            group[s, 0, :, :across] = zero_half
            group[s, planes, :, across:] = zero_half
    for group in (frame, hidden, sdelta, fdelta):
        for s in range(group.shape[0]):
            for p in range(planes + 1):
                group[s, p, :top] = zero_rows
                group[s, p, bottom:] = zero_rows
    for slot in range(2):
        for conv in range(2):
            for piece in range(28, PIECES):
                part[slot, conv, piece] = jnp.zeros((PIECE_ROWS, across), jnp.bfloat16)
    loads[0].wait()
    nothing = jnp.zeros((channels, channels), jnp.float32)
    for conv in range(2):
        for k in range(7):
            wpack[seg, conv, k] = jnp.concatenate(
                [
                    own_ref[conv, 4 * k + g].astype(jnp.float32) if 4 * k + g < 27 else nothing
                    for g in range(4)
                ],
                1,
            ).astype(jnp.bfloat16)

    for load in loads[1:]:
        load.wait()
    size = (rows * channels, channels * planes * rows)
    place = lax.broadcasted_iota(jnp.int32, size, 0)
    origin = (place % channels) * (planes * rows) + place // channels
    source = lax.broadcasted_iota(jnp.int32, size, 1)
    for z in range(planes):
        pick = jnp.where(source == origin + z * rows, 1.0, 0.0).astype(jnp.bfloat16)
        plane = jnp.dot(pick, flat[...], preferred_element_type=jnp.float32).astype(jnp.bfloat16)
        crop_ref[z] = plane[:, :across]
        cot_ref[z] = plane[:, across:]
        put(frame, 0, z, top, plane[:, :across])

    pl.semaphore_wait(barrier, arrivals)

    near, far = 1 - core, core
    deep = HALO * channels

    def halo_copy(group, s, stage, half, pair):
        return pltpu.make_async_remote_copy(
            src_ref=group.at[
                s, pl.ds(2 * pair + 1, 2), pl.ds(pl.multiple_of(top + half * deep, deep), deep),
                pl.ds(0, across),
            ],
            dst_ref=halo.at[stage, 1 - half, pl.ds(2 * pair, 2)],
            send_sem=halo_send.at[stage, half, pair],
            recv_sem=halo_recv.at[stage, 1 - half, pair],
            device_id=(seg, gy - 1 + 2 * half),
            device_id_type=MESH,
        )

    def there(half):
        return (gy - 1 + 2 * half >= 0) & (gy - 1 + 2 * half < count)

    def start_halo(group, s, stage, half, pair):
        @pl.when(there(half))
        def _():
            halo_copy(group, s, stage, half, pair).start()

    def finish_halo(group, s, stage, half):
        @pl.when(there(half))
        def _():
            for pair in range(planes // 2):
                halo_copy(group, s, stage, 1 - half, pair).wait_recv()

        low = pl.multiple_of(half * bottom, channels)
        for z in range(planes):
            put(group, s, z, low, halo[stage, half, z])

    def drain_halo(group, s, stage):
        for half in range(2):
            @pl.when(there(half))
            def _(half=half):
                for pair in range(planes // 2):
                    halo_copy(group, s, stage, half, pair).wait_send()

    half_rows = channels // 2

    def half_of(section, conv, half):
        return wpack.at[section, conv, :, pl.ds(half * half_rows, half_rows)]

    def weight_copy(step, conv, section):
        return pltpu.make_async_remote_copy(
            src_ref=half_of(section, conv, core),
            dst_ref=half_of(section, conv, core),
            send_sem=w_send.at[step - 1, conv],
            recv_sem=w_recv.at[step - 1, conv],
            device_id=((seg + step) % sections, gy),
            device_id_type=MESH,
        )

    def forward_copy(step, conv, half):
        where = half_of((seg - step + sections) % sections, conv, half)
        return pltpu.make_async_remote_copy(
            src_ref=where,
            dst_ref=where,
            send_sem=f_send.at[step - 1, conv],
            recv_sem=f_recv.at[step - 1, conv],
            device_id=(seg, sibling),
            device_id_type=MESH,
        )

    def first_copy(step, conv):
        return pltpu.make_async_remote_copy(
            src_ref=wpack.at[0, conv],
            dst_ref=wpack.at[0, conv],
            send_sem=w_send.at[step - 1, conv],
            recv_sem=w_recv.at[step - 1, conv],
            device_id=((seg + step) % sections, gy),
            device_id_type=MESH,
        )

    def give(s):
        @pl.when(seg == s)
        def _():
            for conv in range(2):
                for step in range(1, sections):
                    if s == 0:
                        first_copy(step, conv).start()
                    else:
                        weight_copy(step, conv, s).start()

    def pass_on(s, conv):
        step = (seg - s + sections) % sections

        @pl.when(step > 0)
        def _():
            weight_copy(step, conv, s).wait_recv()
            forward_copy(step, conv, core).start()

    def arrived(s, conv):
        step = (seg - s + sections) % sections
        if s == 0:
            pl.when(step > 0)(lambda: first_copy(step, conv).wait_recv())
            return

        @pl.when(step > 0)
        def _():
            forward_copy(step, conv, 1 - core).wait_recv()

    give(0)
    for half in (far, near):
        for pair in range(planes // 2):
            start_halo(frame, 0, 0, half, pair)
    give(1)

    lane_group = lax.broadcasted_iota(jnp.int32, (channels, across), 1) // channels
    fold = jnp.where(
        lax.broadcasted_iota(jnp.int32, (channels, across), 0)
        == lax.broadcasted_iota(jnp.int32, (channels, across), 1) % channels,
        1.0,
        0.0,
    ).astype(jnp.bfloat16)

    def compacts(s, direction, conv):
        if direction == 0:
            blocks = []
            for j in range(9):
                for dy in range(4):
                    tap = 9 * (j // 3) + 3 * dy + j % 3
                    blocks.append(
                        jnp.where(
                            lane_group == tap % 4, wpack[s, conv, tap // 4].astype(jnp.float32), 0.0
                        ).astype(jnp.bfloat16)
                        if dy < 3
                        else jnp.zeros((channels, across), jnp.bfloat16)
                    )
            wide = lax.dot_general(
                fold, jnp.concatenate(blocks, 0), (((1,), (1,)), ((), ())),
                preferred_element_type=jnp.float32,
            )
            return [wide[:, j * across : (j + 1) * across] for j in range(9)]
        found = []
        for j in range(9):
            row = jnp.zeros((channels, across), jnp.float32)
            for dy in range(3):
                tap = 26 - (9 * (j // 3) + 3 * dy + j % 3)
                block = wpack[s, conv, tap // 4].astype(jnp.float32)
                by = (dy - tap % 4) % 4
                moved = pltpu.roll(block, by * channels, 1) if by else block
                row = jnp.where(lane_group == dy, moved, row)
            found.append(row)
        return found

    def build(s, direction, conv):
        into = taps.at[s, direction, conv]
        for j, compact in enumerate(compacts(s, direction, conv)):
            dz, dx = j // 3, j % 3
            wide = jnp.concatenate([compact, jnp.zeros_like(compact)], 1)
            for y in range(inner):
                moved = wide if y == 0 else pltpu.roll(wide, y * channels, 1)
                row = (3 * y + dx) * channels
                into[row : row + channels, dz * 2 * across : (dz + 1) * 2 * across] = (
                    moved.astype(jnp.bfloat16)
                )

    def convolve(s, direction, conv, group, index, pair, start):
        at = pl.ds(pl.multiple_of(start * (3 * channels), 3 * channels), 2 * 3 * channels)
        matrix = taps[s, direction, conv, at, :]
        span = group.shape[-2]
        stacked = group[index, 2 * pair : 2 * pair + 3].reshape(3 * span, 2 * across)
        full = jnp.dot(matrix, stacked, preferred_element_type=jnp.float32)
        full = full.reshape(2, 3, channels, 2 * across)
        halves = []
        for half in range(2):
            a, b, c = (
                full[:, dx, :, half * across : (half + 1) * across].reshape(2 * channels, across)
                for dx in range(3)
            )
            halves.append(shifted(a, 1) + b + shifted(c, -1))
        return halves

    inside_low = jnp.where(gy == 0, HALO, 0)
    inside_high = jnp.where(gy == count - 1, rows + HALO, rows + 2 * HALO)
    row_of = lax.broadcasted_iota(jnp.int32, (2 * channels, across), 0) // channels

    def inside(start):
        at = row_of + (start + 1)
        return (at >= inside_low) & (at < inside_high)

    def weight_terms(slot, conv, group, s, delta_group, index):
        for z in range(planes):
            delta = delta_group[index, z + 1, top:bottom, :across].astype(jnp.float32)
            for dx, field in enumerate((shifted(delta, -1), delta, shifted(delta, 1))):
                shifts[
                    dx * rows * channels : (dx + 1) * rows * channels,
                    z * across : (z + 1) * across,
                ] = field.astype(jnp.bfloat16)
        lane = lane_group
        fields = []
        for dz in range(3):
            total = lax.dot_general(
                jnp.concatenate(
                    [
                        group[s, z + dz, channels : (inner + 1) * channels, :]
                        for z in range(0, planes, 2)
                    ],
                    1,
                ),
                shifts[...],
                (((1,), (1,)), ((), ())),
                preferred_element_type=jnp.float32,
            )
            for dy in range(3):
                for dx in range(3):
                    picked = None
                    for y in range(rows):
                        block = total[
                            (y + dy) * channels : (y + dy + 1) * channels,
                            dx * rows * channels : (dx + 1) * rows * channels,
                        ]
                        picked = block if picked is None else jnp.where(lane == y, block, picked)
                    fields.append(picked)
        fields.append(jnp.zeros((channels, across), jnp.float32))
        first_half = lane < 2
        even = lane % 2 == 0
        half = across // 2
        for k in range(7):
            r = fields[4 * k : 4 * k + 4]
            pairs = [
                jnp.where(first_half, r[i], r[i + 2])
                + pltpu.roll(jnp.where(first_half, r[i + 2], r[i]), half, 1)
                for i in range(2)
            ]
            packed = jnp.where(
                even,
                pairs[0] + pltpu.roll(pairs[0], across - channels, 1),
                pairs[1] + pltpu.roll(pairs[1], channels, 1),
            ).astype(jnp.bfloat16)
            for piece in range(4):
                part[slot, conv, 4 * k + piece] = packed[
                    piece * PIECE_ROWS : (piece + 1) * PIECE_ROWS
                ]

    def out_copy(source, into, kind):
        return pltpu.make_async_remote_copy(
            src_ref=source.at[partner],
            dst_ref=into.at[micro],
            send_sem=out_send.at[kind],
            recv_sem=out_recv.at[kind],
            device_id=(partner, gy),
            device_id_type=MESH,
        )

    me = micro * count + gy
    peers = [(gy + d) % count for d in range(1, count)]

    def share_copy(slot, conv, peer, source=None):
        source = me if source is None else source
        return pltpu.make_async_remote_copy(
            src_ref=part.at[slot, conv, pl.ds(peer * share, share)],
            dst_ref=gathered.at[conv, source],
            send_sem=rs_send.at[conv, slot * count + peer],
            recv_sem=rs_recv.at[conv, source],
            device_id=(2 * upper + slot, peer),
            device_id_type=MESH,
        )

    def send_shares(slot, conv):
        for peer in peers:
            share_copy(slot, conv, peer).start()

        @pl.when(micro != slot)
        def _():
            share_copy(slot, conv, gy).start()

    def whole_copy(conv, peer, owner):
        where = reduced.at[conv, pl.ds(owner * share, share)]
        return pltpu.make_async_remote_copy(
            src_ref=where,
            dst_ref=where,
            send_sem=ag_send.at[conv, peer],
            recv_sem=ag_recv.at[conv, owner],
            device_id=(seg, peer),
            device_id_type=MESH,
        )

    def collect(conv):
        total = part[micro, conv, pl.ds(gy * share, share)].astype(jnp.float32)
        senders = [(1 - micro) * count + gy]
        for peer in peers:
            senders += [peer, count + peer]
        for sender in senders:
            share_copy(1 - micro, conv, gy, sender).wait_recv()
            total = total + gathered[conv, sender].astype(jnp.float32)
        reduced[conv, pl.ds(gy * share, share)] = total.astype(jnp.bfloat16)
        for peer in peers:
            whole_copy(conv, peer, gy).start()

    def rows_at(start):
        return pl.ds(pl.multiple_of(start * channels, channels), 2 * channels)

    def forward_first(s, start):
        mask = inside(start)
        for pair in range(planes // 2):
            for half, pre in enumerate(convolve(s, 0, 0, frame, s, pair, start)):
                z = 2 * pair + half
                logistic = logistic_of(pre)
                put(
                    hidden, s, z, pl.multiple_of((start + 1) * channels, channels),
                    jnp.where(mask, pre * logistic, 0.0).astype(jnp.bfloat16),
                )
                slope1[s, z, rows_at(start)] = logistic * (1.0 + pre * (1.0 - logistic))

    def forward_second(s, side):
        at = rows_at(2 * side)
        low = pl.multiple_of(top + side * deep, deep)
        for pair in range(planes // 2):
            for half, pre in enumerate(convolve(s, 0, 1, hidden, s, pair, 1 + 2 * side)):
                z = 2 * pair + half
                logistic = logistic_of(pre)
                slope = logistic * (1.0 + pre * (1.0 - logistic))
                leaving = (pre * logistic).astype(jnp.bfloat16)
                feats[s, z, at] = leaving
                if s + 1 == sections:
                    second = (cot_ref[z, at].astype(jnp.float32) * slope).astype(jnp.bfloat16)
                    put(sdelta, s, z, low, second)
                    continue
                slope2[s, z, at] = slope
                if s in (1, 2):
                    skip = feats[0, z, at] if s == 1 else crop_ref[z, at]
                    leaving = (
                        leaving.astype(jnp.float32) + skip.astype(jnp.float32)
                    ).astype(jnp.bfloat16)
                put(frame, s + 1, z, low, leaving)
            if s + 1 == sections:
                start_halo(sdelta, s, sections + s, side, pair)
            else:
                start_halo(frame, s + 1, s + 1, side, pair)

    def backward_first(s, start):
        mask = inside(start)
        for pair in range(planes // 2):
            for half, pre in enumerate(convolve(s, 1, 1, sdelta, s, pair, start)):
                z = 2 * pair + half
                put(
                    fdelta, s % 2, z, pl.multiple_of((start + 1) * channels, channels),
                    jnp.where(mask, pre * slope1[s, z, rows_at(start)], 0.0).astype(jnp.bfloat16),
                )

    def backward_second(s, side):
        at = rows_at(2 * side)
        low = pl.multiple_of(top + side * deep, deep)
        for pair in range(planes // 2):
            for half, pre in enumerate(convolve(s, 1, 0, fdelta, s % 2, pair, 1 + 2 * side)):
                z = 2 * pair + half
                value = pre.astype(jnp.bfloat16)
                if s < 2:
                    value = (
                        value.astype(jnp.float32) + grads[3 - s, z, at].astype(jnp.float32)
                    ).astype(jnp.bfloat16)
                grads[s, z, at] = value
                if s > 0:
                    put(
                        sdelta, s - 1, z, low,
                        (value.astype(jnp.float32) * slope2[s - 1, z, at]).astype(jnp.bfloat16),
                    )
            if s > 0:
                start_halo(sdelta, s - 1, sections + s - 1, side, pair)

    for s in range(sections):
        if s + 1 < sections and s > 0:
            for conv in range(2):
                pass_on(s + 1, conv)
        arrived(s, 0)
        build(s, 0, 0)
        forward_first(s, 2)
        finish_halo(frame, s, s, near)
        forward_first(s, 4 * near)
        arrived(s, 1)
        build(s, 0, 1)
        if s == 0:
            for later in range(2, sections):
                give(later)
        forward_second(s, near)
        if s > 0:
            tell()
        finish_halo(frame, s, s, far)
        forward_first(s, 4 * far)
        if s == 0:
            for conv in range(2):
                pass_on(1, conv)
        forward_second(s, far)
        tell()

    out_copy(feats, feat_out, 0).start()
    feat_out[micro] = feats[seg]
    for s in reversed(range(sections)):
        build(s, 1, 1)
        backward_first(s, 2)
        finish_halo(sdelta, s, sections + s, near)
        backward_first(s, 4 * near)
        build(s, 1, 0)
        backward_second(s, near)
        if s + 1 < sections:
            @pl.when(upper == (s + 1) // 2)
            def _():
                weight_terms((s + 1) % 2, 0, frame, s + 1, fdelta, (s + 1) % 2)
                send_shares((s + 1) % 2, 0)

        @pl.when(upper == s // 2)
        def _():
            weight_terms(s % 2, 1, hidden, s, sdelta, s)
            send_shares(s % 2, 1)

        finish_halo(sdelta, s, sections + s, far)
        backward_first(s, 4 * far)
        if s == 0:
            @pl.when(upper == 0)
            def _():
                weight_terms(0, 0, frame, 0, fdelta, 0)
                send_shares(0, 0)

        backward_second(s, far)

        @pl.when(partner == s)
        def _():
            out_copy(grads, grad_out, 1).start()

    collect(1)
    grad_out[micro] = grads[seg]
    collect(0)
    for conv in (1, 0):
        for peer in peers:
            whole_copy(conv, peer, peer).wait_recv()

    for kind, (source, into) in enumerate(((feats, feat_out), (grads, grad_out))):
        out_copy(source, into, kind).wait()
    for s in range(sections):
        drain_halo(frame, s, s)
        drain_halo(sdelta, s, sections + s)
    for conv in range(2):
        for step in range(1, sections):
            @pl.when(seg == 0)
            def _():
                first_copy(step, conv).wait_send()

            @pl.when(seg > 0)
            def _():
                weight_copy(step, conv, seg).wait_send()

            @pl.when(seg != step)
            def _():
                forward_copy(step, conv, core).wait_send()
    for conv in range(2):
        for slot in range(2):
            for peer in peers:
                share_copy(slot, conv, peer).wait_send()
        share_copy(1 - micro, conv, gy).wait_send()
        for peer in peers:
            whole_copy(conv, peer, gy).wait_send()


def layout_kernel(
    sizes, feats, grads, reduced, feat_hbm, grad_hbm, wg_hbm, feat_flat, grad_flat, wg_wide, sems
):
    channels, planes, rows, across = sizes
    cells = channels * planes * rows
    place = lax.broadcasted_iota(jnp.int32, (cells, cells), 0)
    source = lax.broadcasted_iota(jnp.int32, (cells, cells), 1)
    wanted = (place % (planes * rows)) * channels + place // (planes * rows)
    pick = jnp.where(source == wanted, 1.0, 0.0).astype(jnp.bfloat16)
    copies = []
    everything = reduced[...].reshape(2, PIECES, PIECE_ROWS, across)
    for conv in range(2):
        for k in range(7):
            block = jnp.concatenate(
                [everything[conv, 4 * k + piece].astype(jnp.float32) for piece in range(4)], 0
            )
            for lane_group in range(4 if k < 6 else 3):
                moved = (
                    pltpu.roll(block, across - lane_group * channels, 1) if lane_group else block
                )
                wg_wide[conv, 4 * k + lane_group] = moved[:, :channels]
        copies.append(pltpu.make_async_copy(wg_wide.at[conv], wg_hbm.at[conv], sems.at[0, conv]))
        copies[-1].start()
    for k, (value, flat, hbm) in enumerate(
        ((grads, grad_flat, grad_hbm), (feats, feat_flat, feat_hbm))
    ):
        for m in range(2):
            flat[m] = jnp.dot(
                pick, value[m].reshape(cells, across), preferred_element_type=jnp.float32
            ).astype(flat.dtype)
            copies.append(pltpu.make_async_copy(flat.at[m], hbm.at[m], sems.at[k + 1, m]))
            copies[-1].start()
    for copy in copies:
        copy.wait()


def local(crops, cotangent, weights):
    micro_count, channels, planes, rows, across = crops.shape
    sizes = (channels, planes, rows, across)
    segment = lax.axis_index("segment")
    sections = lax.axis_size("segment")
    count = lax.axis_size("gy")
    micro = segment % 2
    inner = rows + 2
    span = (rows + 2 * HALO) * channels
    vmem = pl.BlockSpec(memory_space=pltpu.VMEM)
    bf = lambda *shape: pltpu.VMEM(shape, jnp.bfloat16)
    fl = lambda *shape: pltpu.VMEM(shape, jnp.float32)
    dma = lambda *shape: pltpu.SemaphoreType.DMA(shape)

    band = (planes, rows * channels, across)
    double = (planes + 1, span, 2 * across)
    cells = channels * planes * rows
    pieces = (PIECES, PIECE_ROWS, across)
    anywhere = pl.BlockSpec(memory_space=pltpu.HBM)
    shape = jax.ShapeDtypeStruct
    features, grads, reduced = pl.pallas_call(
        functools.partial(network_kernel, sizes, sections, count),
        out_shape=(
            shape((2, *band), jnp.bfloat16),
            shape((2, *band), jnp.bfloat16),
            shape((2, *pieces), jnp.bfloat16),
        ),
        in_specs=[anywhere] * 3,
        out_specs=(vmem,) * 3,
        scratch_shapes=[
            bf(cells, 2 * across),
            bf(2, 27, channels, channels),
            bf(*band),
            bf(*band),
            bf(sections, *double),
            bf(sections, *double),
            bf(sections, *double),
            bf(2, *double),
            fl(sections, planes, inner * channels, across),
            fl(sections, *band),
            bf(sections, *band),
            bf(sections, *band),
            bf(2 * sections, 2, planes, HALO * channels, across),
            bf(sections, 2, 7, channels, across),
            bf(sections, 2, 2, 3 * inner * channels, 3 * span),
            bf(3 * rows * channels, planes * across),
            bf(2, 2, *pieces),
            bf(2, 2 * count, PIECES // count, PIECE_ROWS, across),
            dma(3),
            pltpu.SemaphoreType.REGULAR((2 * sections,)),
            dma(2 * sections, 2, planes // 2),
            dma(2 * sections, 2, planes // 2),
            dma(sections - 1, 2),
            dma(sections - 1, 2),
            dma(sections - 1, 2),
            dma(sections - 1, 2),
            dma(2),
            dma(2),
            dma(2, 2 * count),
            dma(2, 2 * count),
            dma(2, count),
            dma(2, count),
        ],
        compiler_params=pltpu.CompilerParams(
            vmem_limit_bytes=48 * 2**20, collective_id=0, has_side_effects=True
        ),
    )(
        crops.reshape(micro_count, cells, across),
        cotangent.reshape(micro_count, cells, across),
        weights[0],
    )
    features, grads, weight_grads = pl.pallas_call(
        functools.partial(layout_kernel, sizes),
        out_shape=(
            shape((2, cells, across), jnp.bfloat16),
            shape((2, cells, across), jnp.float32),
            shape((2, 27, channels, channels), jnp.float32),
        ),
        in_specs=[vmem] * 3,
        out_specs=(anywhere,) * 3,
        scratch_shapes=[
            bf(2, cells, across),
            fl(2, cells, across),
            fl(2, 27, channels, channels),
            dma(3, 2),
        ],
        compiler_params=pltpu.CompilerParams(vmem_limit_bytes=8 * 2**20),
    )(features, grads, reduced)
    volume = (1, 2, channels, planes, rows, across)
    return features.reshape(volume), weight_grads[None], grads.reshape(volume)


def solution(mesh):
    return jax.shard_map(
        local,
        mesh=mesh,
        in_specs=(
            P(None, None, None, "gy", None),
            P(None, None, None, "gy", None),
            P("segment", None, None, None, None),
        ),
        out_specs=(
            P("segment", None, None, None, "gy", None),
            P("segment", None, None, None, None),
            P("segment", None, None, None, "gy", None),
        ),
        check_vma=False,
    )
```

time: 60.6 us -> 59.3 us (0.979)
  Pallas kernels: 56.7 us -> 55.4 us
    pallas_call x1, Pallas kernels: 55.1 us -> 53.8 us  [local(): pl.pallas_call(functools.partial(network_kernel, sizes, sections, count),...]
where the time goes in v3:
time: 59.3 us; the launch traced here: 59.1 us
  Pallas kernels  55.4 us (93%)
  local copies, waits for them, and re-layouts  2.91 us (5%)
  between operations  0.81 us (1%)
    pallas_call x1, Pallas kernels, local(): pl.pallas_call(functools.partial(network_kernel, sizes, sections, count),...  53.8 us
    unnamed x6, local copies, waits for them, and re-layouts  2.91 us
    pallas_call x1, Pallas kernels, local(): pl.pallas_call(functools.partial(layout_kernel, sizes), out_shape=(shape(...  1.55 us

profile of v3, /device:TPU:0, one launch (start us, length us, event | category | flops | bytes accessed | tf_op | source)
XLA Modules:
  0.0 59.1 jit_solution(17148391295592371809)
XLA Ops:
  0.6 0.0 copy-start
  0.6 1.0 %copy-done = bf16[1,2,27,32,32]{4,3,2,1,0:T(8,128)(2,1)S(1)} copy-done((bf16[1,2,27,32,32]{4,3,2,1,0:T(8,128)(2,1)S(1)}, bf16[1,2,27,32,32]{4,3,2,1,0:T(8,128)(2,1)}, u32[]{:S(2)}) %copy-start) | copy-done | bytes 110616
  1.6 0.0 copy-start.1
  1.6 0.9 %copy-done.1 = bf16[2,32,4,4,128]{4,3,2,1,0:T(4,128)(2,1)S(1)} copy-done((bf16[2,32,4,4,128]{4,3,2,1,0:T(4,128)(2,1)S(1)}, bf16[2,32,4,4,128]{4,3,2,1,0:T(4,128)(2,1)}, u32[]{:S(2)}) %copy-start.1) | copy-done | bytes 262168
  2.6 0.0 copy-start.2
  2.6 0.9 %copy-done.2 = bf16[2,32,4,4,128]{4,3,2,1,0:T(4,128)(2,1)S(1)} copy-done((bf16[2,32,4,4,128]{4,3,2,1,0:T(4,128)(2,1)S(1)}, bf16[2,32,4,4,128]{4,3,2,1,0:T(4,128)(2,1)}, u32[]{:S(2)}) %copy-start.2) | copy-done | bytes 262168
  3.5 53.8 %shard_map.58 = (bf16[2,4,128,128]{3,2,1,0:T(8,128)(2,1)S(1)}, bf16[2,4,128,128]{3,2,1,0:T(8,128)(2,1)S(1)}, bf16[2,32,8,128]{3,2,1,0:T(8,128)(2,1)S(1)}) custom-call(bf16[2,512,128]{2,1,0:T(8,128)(2,1)S(1)} %bitcast.7, bf16[2,512,128]{2,1,0:T(8,128)(2,1)S(1)} %bitcast.8, bf16[2,27,32,32]{3,2,1,0:T(8,128)(2,1)S(1)} %bitcast.6), custom_call_target="tpu_custom_call" | custom-call | tf_op jit(solution)/shard_map/pallas_call | solution.py:707
  57.4 1.6 %shard_map.59 = (bf16[2,512,128]{2,1,0:T(8,128)(2,1)}, f32[2,512,128]{2,1,0:T(8,128)}, f32[2,27,32,32]{3,2,1,0:T(8,128)}) custom-call(bf16[2,4,128,128]{3,2,1,0:T(8,128)(2,1)S(1)} %get-tuple-element.9.feats, bf16[2,4,128,128]{3,2,1,0:T(8,128)(2,1)S(1)} %get-tuple-element.10.grads, bf16[2,32,8,128]{3,2,1,0:T(8,128)(2,1)S(1)} %get-tuple-element.11.reduced), custom_call_target="tpu_custom_call" | custom-call | tf_op jit(solution)/shard_map/pallas_call | solution.py:758
Async XLA Ops:
  0.6 1.0 %copy-start = (bf16[1,2,27,32,32]{4,3,2,1,0:T(8,128)(2,1)S(1)}, bf16[1,2,27,32,32]{4,3,2,1,0:T(8,128)(2,1)}, u32[]{:S(2)}) copy-start(bf16[1,2,27,32,32]{4,3,2,1,0:T(8,128)(2,1)} %param.5) | copy-start | bytes 331780
  1.6 0.9 %copy-start.1 = (bf16[2,32,4,4,128]{4,3,2,1,0:T(4,128)(2,1)S(1)}, bf16[2,32,4,4,128]{4,3,2,1,0:T(4,128)(2,1)}, u32[]{:S(2)}) copy-start(bf16[2,32,4,4,128]{4,3,2,1,0:T(4,128)(2,1)} %param.3) | copy-start | bytes 786436
  2.6 0.9 %copy-start.2 = (bf16[2,32,4,4,128]{4,3,2,1,0:T(4,128)(2,1)S(1)}, bf16[2,32,4,4,128]{4,3,2,1,0:T(4,128)(2,1)}, u32[]{:S(2)}) copy-start(bf16[2,32,4,4,128]{4,3,2,1,0:T(4,128)(2,1)} %param.4) | copy-start | bytes 786436

commit v4 on v3

--- a/solution.py
+++ b/solution.py
@@ -751,9 +751,9 @@
             vmem_limit_bytes=48 * 2**20, collective_id=0, has_side_effects=True
         ),
     )(
-        crops.reshape(micro_count, cells, across),
-        cotangent.reshape(micro_count, cells, across),
-        weights[0],
+        pltpu.with_memory_space_constraint(crops.reshape(micro_count, cells, across), pltpu.HBM),
+        pltpu.with_memory_space_constraint(cotangent.reshape(micro_count, cells, across), pltpu.HBM),
+        pltpu.with_memory_space_constraint(weights[0], pltpu.HBM),
     )
     features, grads, weight_grads = pl.pallas_call(
         functools.partial(layout_kernel, sizes),

time: 59.3 us -> 56.1 us (0.946)
  local copies, waits for them, and re-layouts: 2.91 us -> 0 us
    unnamed x6 -> x0, local copies, waits for them, and re-layouts: 2.91 us -> none
where the time goes in v4:
time: 56.1 us; the launch traced here: 55.9 us
  Pallas kernels  55.1 us (98%)
  between operations  0.8 us (1%)
    pallas_call x1, Pallas kernels, local(): pl.pallas_call(functools.partial(network_kernel, sizes, sections, count),...  53.6 us
    pallas_call x1, Pallas kernels, local(): pl.pallas_call(functools.partial(layout_kernel, sizes), out_shape=(shape(...  1.56 us

profile of v4, /device:TPU:0, one launch (start us, length us, event | category | flops | bytes accessed | tf_op | source)
XLA Modules:
  0.0 55.9 jit_solution(10826885446979885062)
XLA Ops:
  0.6 53.6 %shard_map.58 = (bf16[2,4,128,128]{3,2,1,0:T(8,128)(2,1)S(1)}, bf16[2,4,128,128]{3,2,1,0:T(8,128)(2,1)S(1)}, bf16[2,32,8,128]{3,2,1,0:T(8,128)(2,1)S(1)}) custom-call(bf16[2,512,128]{2,1,0:T(8,128)(2,1)} %bitcast.7, bf16[2,512,128]{2,1,0:T(8,128)(2,1)} %bitcast.8, bf16[2,27,32,32]{3,2,1,0:T(8,128)(2,1)} %bitcast.6), custom_call_target="tpu_custom_call" | custom-call | tf_op jit(solution)/shard_map/pallas_call | solution.py:707
  54.2 1.6 %shard_map.59 = (bf16[2,512,128]{2,1,0:T(8,128)(2,1)}, f32[2,512,128]{2,1,0:T(8,128)}, f32[2,27,32,32]{3,2,1,0:T(8,128)}) custom-call(bf16[2,4,128,128]{3,2,1,0:T(8,128)(2,1)S(1)} %get-tuple-element.9.feats, bf16[2,4,128,128]{3,2,1,0:T(8,128)(2,1)S(1)} %get-tuple-element.10.grads, bf16[2,32,8,128]{3,2,1,0:T(8,128)(2,1)S(1)} %get-tuple-element.11.reduced), custom_call_target="tpu_custom_call" | custom-call | tf_op jit(solution)/shard_map/pallas_call | solution.py:758
